TPU v7x, 32 devices: a whole 2x2x4 slice. The times are simulated.
32 devices in a mesh: section: 2 (over y), dp: 16 (over z, x, core).
Axes of the slice: x: 2, y: 2, z: 4, core: 2. Of those that a mesh axis runs over, the one named last changes fastest.
Arguments:
- activations: bfloat16 [2, 4, 16, 14336], P('section', None, 'dp'), may hold values from -6 to 6
- out_grads: bfloat16 [2, 4, 16, 4096], P('section', None, 'dp'), may hold values from -6 to 6
- basis_in: bfloat16 [2, 14336, 1024], P('section', 'dp'), may hold values from -0.046875 to 0.046875
- basis_out: bfloat16 [2, 4096, 1024], P('section', 'dp'), may hold values from -0.09375 to 0.09375
- eigen_values: float32 [2, 1024, 1024], P('section', 'dp'), may hold values from 0.02 to 2
- query_proj: bfloat16 [2, 8, 1024, 1024], P('section', None, 'dp'), may hold values from -0.046875 to 0.046875
- lengths: int32 [4], replicated, may hold values from 4 to 16
- seq_rows: int32 [4], replicated, may hold values from 0 to 127
- prior_table: float32 [128, 8], P('dp'), may hold values from -6 to 6
Outputs:
- influence: float32 [2, 128, 8], P('section', 'dp')
All inputs are finite; a program needn't handle non-finite values.
Results may differ from a plain program's by a relative error of at most 0.01.
Values may be sent and summed in bfloat16 or wider, within the bound.
No kernel may reach another device: no remote copies, remote signals or barrier semaphores. Data moves between devices by JAX's collectives and lax.ppermute only.
A program may use at most 64 MiB of HBM per device.

v0:
```python
import jax
import jax.numpy as jnp
from jax import lax
from jax.sharding import PartitionSpec as P

DAMPING = 0.01


def entering(value, axis, join, neutral):
    count, mine = (lax.axis_size(axis), lax.axis_index(axis))
    pieces = lax.all_gather(value, axis)
    running = jnp.full_like(value, 0) + jnp.asarray(neutral, value.dtype)

    def step(position, running):
        longer = join(running, pieces[position])
        return jnp.where(position < mine, longer, running)

    return lax.fori_loop(0, count - 1, step, running)


def add_pair(earlier, latter):
    return earlier + latter


def per_device(
    activations,
    out_grads,
    basis_in,
    basis_out,
    eigen_values,
    query_proj,
    lengths,
    seq_rows,
    prior_table,
):
    micro = activations.shape[1]
    cols_acts, cols_grads = (
        lax.all_to_all(activations[0], "dp", split_axis=2, concat_axis=1, tiled=True),
        lax.all_to_all(out_grads[0], "dp", split_axis=2, concat_axis=1, tiled=True),
    )
    slots = cols_acts.shape[1]
    rank_size = basis_in.shape[2]
    act_part = jnp.dot(
        cols_acts.reshape(micro * slots, cols_acts.shape[2]),
        basis_in[0],
        preferred_element_type=jnp.float32,
    )
    grad_part = jnp.dot(
        cols_grads.reshape(micro * slots, cols_grads.shape[2]),
        basis_out[0],
        preferred_element_type=jnp.float32,
    )
    grad_share = lax.psum_scatter(grad_part, "dp", scatter_dimension=1, tiled=True).astype(
        jnp.bfloat16
    )
    act_proj = lax.psum(act_part, "dp").astype(jnp.bfloat16)
    block_rows = grad_share.shape[1]
    position = jnp.arange(slots, dtype=jnp.int32)
    live_mask = (position[None, :] < lengths[:, None]).reshape(micro * slots, 1)
    grad_share = jnp.where(live_mask, grad_share, jnp.zeros_like(grad_share))
    inverse_len = 1.0 / lengths.astype(jnp.float32)
    seq_block = (
        jnp.einsum(
            "mti,mtj->mij",
            grad_share.reshape(micro, slots, block_rows),
            act_proj.reshape(micro, slots, rank_size),
            preferred_element_type=jnp.float32,
        )
        * inverse_len[:, None, None]
    )
    precond = (query_proj[0].astype(jnp.float32) / (eigen_values[0][None] + DAMPING)).astype(
        jnp.bfloat16
    )
    partial_value = jnp.einsum(
        "mij,qij->mq", seq_block, precond.astype(jnp.float32), precision=lax.Precision.HIGHEST
    )
    table_rows = prior_table.shape[0]
    first_row = lax.axis_index("dp") * table_rows
    summed = lax.psum(partial_value, "dp")
    before = entering(summed, "section", add_pair, jnp.zeros_like(summed))
    owner_mask = (
        seq_rows[None, :] == (first_row + jnp.arange(table_rows, dtype=jnp.int32))[:, None]
    ).astype(jnp.float32)
    result = prior_table + jnp.dot(owner_mask, before + summed, precision=lax.Precision.HIGHEST)
    return result[None]


def solution(mesh):
    return jax.shard_map(
        per_device,
        mesh=mesh,
        in_specs=(
            P("section", None, "dp", None),
            P("section", None, "dp", None),
            P("section", "dp", None),
            P("section", "dp", None),
            P("section", "dp", None),
            P("section", None, "dp", None),
            P(),
            P(),
            P("dp", None),
        ),
        out_specs=P("section", "dp", None),
        check_vma=False,
    )
```

profile of v0, /device:TPU:0, one launch (start us, length us, event | category | flops | bytes accessed | tf_op | source)
XLA Modules:
  0.0 303.3 jit_solution(3628222360008374152)
XLA Ops:
  6.5 0.0 copy-start
  6.5 5.0 %copy.14 = bf16[4,1,4096]{0,1,2:T(2,128)(2,1)} copy(bf16[4,1,4096]{2,0,1:T(4,128)(2,1)} %bitcast.47) | data formatting | bytes 65536 | tf_op jit(solution)/shard_map/squeeze | solution.py:39
  11.5 0.5 broadcast.36
  12.1 0.0 copy-start.7
  12.1 0.0 copy-start.3
  12.1 23.5 %reduce = bf16[4096,4]{1,0:T(8,128)(2,1)S(1)} reduce(bf16[4096,1,4]{2,1,0:T(2,128)(2,1)} %bitcast.42, bf16[]{:T(256)} %broadcast.36), dimensions={1}, to_apply=%bitcast.32.reduce_sub_computation | reduce | bytes 65538
  35.5 2.6 reshape.67
  38.1 7.4 %all-to-all-start = ((bf16[16,2,512]{2,1,0:T(2,128)(2,1)}), bf16[16,2,512]{2,1,0:T(2,128)(2,1)S(1)}, u32[]{:S(2)}, u32[]{:S(2)}) async-start(bf16[16,2,512]{2,1,0:T(2,128)(2,1)} %reshape.67), calls=%async_computation | async-start | bytes 65536 | tf_op jit(solution)/shard_map/all_to_all | solution.py:39
  45.5 0.0 copy-done.7
  45.6 0.1 iota_compare_fusion
  45.6 0.5 convert_divide_fusion.1
  46.2 0.0 copy-done.3
  46.2 11.6 %copy.16 = bf16[4,1,14336]{0,1,2:T(2,128)(2,1)} copy(bf16[4,1,14336]{2,0,1:T(4,128)(2,1)S(1)} %bitcast.45) | data formatting | bytes 229376 | tf_op jit(solution)/shard_map/squeeze | solution.py:38
  57.7 79.8 %reduce.1 = bf16[14336,4]{1,0:T(8,128)(2,1)} reduce(bf16[14336,1,4]{2,1,0:T(2,128)(2,1)} %bitcast.41, bf16[]{:T(256)} %broadcast.36), dimensions={1}, to_apply=%bitcast.34.reduce_sub_computation | reduce | bytes 229378
  137.6 0.0 copy-start.2
  137.6 8.3 %reshape.69 = bf16[16,2,1792]{2,1,0:T(2,128)(2,1)} reshape(bf16[14336,4]{1,0:T(8,128)(2,1)} %reduce.1) | data formatting | bytes 229376
  145.8 0.6 lt.31
  146.4 0.0 copy-done.2
  146.5 1.5 fusion
  148.0 0.5 iota_add_fusion
  148.6 0.0 all-to-all-done
  148.6 6.0 %all-to-all-start.1 = ((bf16[16,2,1792]{2,1,0:T(2,128)(2,1)}), bf16[16,2,1792]{2,1,0:T(2,128)(2,1)S(1)}, u32[]{:S(2)}, u32[]{:S(2)}) async-start(bf16[16,2,1792]{2,1,0:T(2,128)(2,1)} %reshape.69), calls=%async_computation.1 | async-start | bytes 229376 | tf_op jit(solution)/shard_map/all_to_all | solution.py:38
  154.6 0.0 copy-start.1
  154.6 0.0 reduce-scatter.4.cloned.1.call-start
  154.6 4.5 %reshape.68 = bf16[4096,1,4]{2,1,0:T(2,128)(2,1)} reshape(bf16[16,2,512]{2,1,0:T(2,128)(2,1)S(1)} %all-to-all-done) | data formatting | bytes 65536
  159.2 4.5 %copy.15 = bf16[4,1,4096]{2,0,1:T(4,128)(2,1)S(1)} copy(bf16[4,1,4096]{0,1,2:T(2,128)(2,1)} %bitcast.43) | data formatting | bytes 65536 | tf_op jit(solution)/shard_map/all_to_all | solution.py:39
  163.7 0.6 reshape.47
  164.3 0.0 copy-done.1
  164.4 1.9 convolution_bitcast_fusion
  166.2 0.0 reduce-scatter.4.cloned.1.call-update
  166.3 0.0 all-to-all-done.1
  166.3 11.5 %reshape.70 = bf16[14336,1,4]{2,1,0:T(2,128)(2,1)} reshape(bf16[16,2,1792]{2,1,0:T(2,128)(2,1)S(1)} %all-to-all-done.1) | data formatting | bytes 229376
  177.8 13.9 %copy.17 = bf16[4,1,14336]{2,0,1:T(4,128)(2,1)S(1)} copy(bf16[4,1,14336]{0,1,2:T(2,128)(2,1)} %bitcast.40) | data formatting | bytes 229376 | tf_op jit(solution)/shard_map/all_to_all | solution.py:38
  191.7 0.0 copy-start.5
  191.7 0.0 copy-start.4
  191.8 0.1 reshape.49
  191.8 0.0 copy-done
  191.9 0.4 fusion.1
  192.3 0.0 copy-start.6
  192.3 0.0 copy-start.8
  192.3 0.0 copy-start.9
  192.3 64.6 %all-reduce.1 = bf16[64,1024]{1,0:T(8,128)(2,1)S(1)} all-reduce(f32[64,1024]{1,0:T(8,128)S(1)} %fusion.1), channel_id=1, replica_groups=mesh['section'=2,'dp'=16] {'dp'}, use_global_device_ids=true, to_apply=%region_1.0 | all-reduce | flops 65536 | bytes 393216 | tf_op jit(solution)/shard_map/psum | solution.py:56
  256.9 0.0 reduce-scatter.4.cloned.1.call-done
  257.0 0.8 copy.21
  257.8 0.0 copy-done.5
  257.8 0.1 convert_select_fusion
  257.9 0.0 copy-done.4
  257.9 0.3 convolution_multiply_fusion
  258.3 3.5 %convolution_bitcast_fusion.1 = f32[4,8]{1,0:T(4,128)S(1)} fusion(bf16[8,64,1024]{2,1,0:T(8,128)(2,1)S(1)} %fusion, f32[4,64,1024]{2,1,0:T(8,128)S(1)} %convolution_multiply_fusion), kind=kOutput, calls=%fused_computation.8 | convolution fusion | flops 25165824 | bytes 2097280 | tf_op jit(solution)/shard_map/mij,qij->mq/dot_general | solution.py:74
  261.8 29.5 %psum.15 = f32[4,8]{1,0:T(4,128)S(1)} all-reduce(f32[4,8]{1,0:T(4,128)S(1)} %convolution_bitcast_fusion.1), channel_id=1, replica_groups=mesh['section'=2,'dp'=16] {'dp'}, use_global_device_ids=true, to_apply=%region_2.3 | all-reduce | flops 32 | bytes 256 | tf_op jit(solution)/shard_map/psum | solution.py:79
  291.3 4.4 %all-gather.1 = f32[2,4,8]{2,1,0:T(4,128)S(1)} all-gather(f32[1,4,8]{2,1,0:T(4,128)S(1)} %bitcast.49), channel_id=2, replica_groups=mesh['section'=2,'dp'=16] {'section'}, dimensions={0}, use_global_device_ids=true | all-gather | bytes 384 | tf_op jit(solution)/shard_map/all_gather | solution.py:11
  295.6 0.0 copy-done.6
  295.6 0.0 copy-done.8
  295.6 0.0 copy-done.9
  295.6 0.8 fusion.3
  (1 shorter events, 0.0 us)
Async XLA Ops:
  6.5 185.3 %copy-start = (bf16[1,896,1024]{2,1,0:T(8,128)(2,1)S(1)}, bf16[1,896,1024]{2,1,0:T(8,128)(2,1)}, u32[]{:S(2)}) copy-start(bf16[1,896,1024]{2,1,0:T(8,128)(2,1)} %param.11) | copy-start | bytes 5505028
  12.1 33.5 %copy-start.7 = (s32[4]{0:T(128)S(1)}, s32[4]{0:T(128)}, u32[]{:S(2)}) copy-start(s32[4]{0:T(128)} %param.15) | copy-start | bytes 52
  12.1 34.1 %copy-start.3 = (bf16[1,4,1,14336]{3,1,2,0:T(4,128)(2,1)S(1)}, bf16[1,4,1,14336]{3,1,2,0:T(4,128)(2,1)}, u32[]{:S(2)}) copy-start(bf16[1,4,1,14336]{3,1,2,0:T(4,128)(2,1)} %param.9) | copy-start | bytes 344068
  38.1 110.4 %all-to-all-start = ((bf16[16,2,512]{2,1,0:T(2,128)(2,1)}), bf16[16,2,512]{2,1,0:T(2,128)(2,1)S(1)}, u32[]{:S(2)}, u32[]{:S(2)}) async-start(bf16[16,2,512]{2,1,0:T(2,128)(2,1)} %reshape.67), calls=%async_computation | async-start | bytes 65536 | tf_op jit(solution)/shard_map/all_to_all | solution.py:39
  137.6 8.9 %copy-start.2 = (f32[1,64,1024]{2,1,0:T(8,128)S(1)}, f32[1,64,1024]{2,1,0:T(8,128)}, u32[]{:S(2)}) copy-start(f32[1,64,1024]{2,1,0:T(8,128)} %param.13) | copy-start | bytes 786436
  148.6 17.7 %all-to-all-start.1 = ((bf16[16,2,1792]{2,1,0:T(2,128)(2,1)}), bf16[16,2,1792]{2,1,0:T(2,128)(2,1)S(1)}, u32[]{:S(2)}, u32[]{:S(2)}) async-start(bf16[16,2,1792]{2,1,0:T(2,128)(2,1)} %reshape.69), calls=%async_computation.1 | async-start | bytes 229376 | tf_op jit(solution)/shard_map/all_to_all | solution.py:38
  154.6 9.8 %copy-start.1 = (bf16[1,256,1024]{2,1,0:T(8,128)(2,1)S(1)}, bf16[1,256,1024]{2,1,0:T(8,128)(2,1)}, u32[]{:S(2)}) copy-start(bf16[1,256,1024]{2,1,0:T(8,128)(2,1)} %param.12) | copy-start | bytes 1572868
  154.6 102.4 %reduce-scatter.4.cloned.1.call-start = ((), (), s32[]{:S(2)}) async-start(), calls=%async_computation.3 | async-start | bytes 557056
  191.7 66.1 %copy-start.5 = (pred[64]{0:T(512)(128)(4,1)S(1)}, pred[64]{0:T(512)(128)(4,1)}, u32[]{:S(2)}) copy-start(pred[64]{0:T(512)(128)(4,1)} %lt.31) | copy-start | bytes 196
  191.7 66.1 %copy-start.4 = (f32[4]{0:T(128)S(1)}, f32[4]{0:T(128)}, u32[]{:S(2)}) copy-start(f32[4]{0:T(128)} %convert_divide_fusion.1) | copy-start | bytes 52
  192.3 103.3 %copy-start.6 = (f32[8,8]{1,0:T(8,128)S(1)}, f32[8,8]{1,0:T(8,128)}, u32[]{:S(2)}) copy-start(f32[8,8]{1,0:T(8,128)} %param.17) | copy-start | bytes 772
  192.3 103.3 %copy-start.8 = (s32[4]{0:T(128)S(1)}, s32[4]{0:T(128)}, u32[]{:S(2)}) copy-start(s32[4]{0:T(128)} %param.16) | copy-start | bytes 52
  192.3 103.3 %copy-start.9 = (s32[8]{0:T(128)S(1)}, s32[8]{0:T(128)}, u32[]{:S(2)}) copy-start(s32[8]{0:T(128)} %iota_add_fusion) | copy-start | bytes 100
Sparse Core Ops, SparseCore 0:
  166.4 57.5 reduce-scatter.3
where the time goes:
time: 304 us; the launch traced here: 303 us
  other arithmetic  106 us (35%)
  blocking collectives  98.4 us (32%)
  local copies, waits for them, and re-layouts  64.7 us (21%)
  between operations  13.6 us (4%)
  starting transfers between devices  13.4 us (4%)
  matrix products  6.96 us (2%)
    unnamed x2, other arithmetic  103 us
    psum x1, blocking collectives, per_device(): act_proj = lax.psum(act_part, 'dp').astype(jnp.bfloat16)  64.6 us
    psum x1, blocking collectives, per_device(): summed = lax.psum(partial_value, 'dp')  29.5 us
    unnamed x26, local copies, waits for them, and re-layouts  28.3 us
    all_to_all x1, local copies, waits for them, and re-layouts, per_device(): lax.all_to_all(activations[0], 'dp', split_axis=2, concat_axis=1, tiled=T...  13.9 us
    squeeze x1, local copies, waits for them, and re-layouts, per_device(): activations[0]  11.6 us
    all_to_all x1, starting transfers between devices, per_device(): lax.all_to_all(out_grads[0], 'dp', split_axis=2, concat_axis=1, tiled=True)  7.39 us
  transfers between devices with their start and end apart: 3, of which 0 were waited for; matrix products, arithmetic and copies ran while one was open for 46% of the time, Pallas kernels for 0%

commit v1 on v0

v1 whole, which is shorter than its diff:
```python
import jax
import jax.numpy as jnp
from jax import lax
from jax.sharding import PartitionSpec as P

DAMPING = 0.01
F32 = jnp.float32
BF16 = jnp.bfloat16


def exchange(pieces, axes):
    return lax.all_to_all(pieces, axes, split_axis=0, concat_axis=0, tiled=True)


def per_device(
    activations,
    out_grads,
    basis_in,
    basis_out,
    eigen_values,
    query_proj,
    lengths,
    seq_rows,
    prior_table,
):
    n = lax.axis_size("dp")
    sections = lax.axis_size("section")
    micro, own_slots, hidden = activations.shape[1:]
    features = out_grads.shape[3]
    hidden_share, feature_share = hidden // n, features // n
    own_rows = micro * own_slots
    rows = n * own_rows
    rank = basis_in.shape[2]
    share = rank // n
    queries = query_proj.shape[1]

    pieces = jnp.concatenate(
        [
            activations[0].reshape(own_rows, n, hidden_share),
            out_grads[0].reshape(own_rows, n, feature_share),
        ],
        axis=2,
    ).transpose(1, 0, 2)
    got = exchange(pieces, "dp").reshape(rows, hidden_share + feature_share)

    act_part = jnp.dot(got[:, :hidden_share], basis_in[0], preferred_element_type=F32)
    grad_part = jnp.dot(got[:, hidden_share:], basis_out[0], preferred_element_type=F32)
    parts = jnp.concatenate(
        [
            act_part.astype(BF16).reshape(rows, n, share),
            grad_part.astype(BF16).reshape(rows, n, share),
        ],
        axis=2,
    ).transpose(1, 0, 2)
    sums = jnp.sum(exchange(parts, "dp").astype(F32), axis=0)
    act_own = sums[:, :share].astype(BF16)

    row = jnp.arange(rows, dtype=jnp.int32)
    row_micro = (row // own_slots) % micro
    row_slot = (row // own_rows) * own_slots + row % own_slots
    micro_mask = row_micro[None, :] == jnp.arange(micro, dtype=jnp.int32)[:, None]
    live = jnp.any(micro_mask & (row_slot[None, :] < lengths[:, None]), axis=0)
    grad_own = jnp.where(live[:, None], sums[:, share:], 0.0).astype(BF16)

    act_all = exchange(jnp.broadcast_to(act_own[None], (n, rows, share)), "dp")
    act_proj = act_all.transpose(1, 0, 2).reshape(rows, rank)

    precond = (query_proj[0].astype(F32) / (eigen_values[0][None] + DAMPING)).astype(BF16)
    turned = jnp.einsum("ri,qij->qrj", grad_own, precond, preferred_element_type=F32)
    per_row = jnp.sum(turned * act_proj.astype(F32)[None], axis=2)
    weight = micro_mask.astype(F32) / lengths.astype(F32)[:, None]
    partial = jnp.sum(per_row[None] * weight[:, None, :], axis=2)

    total = n * sections
    spread = jnp.broadcast_to(partial.reshape(1, 1, micro * queries), (total, 1, micro * queries))
    scores = exchange(spread, ("section", "dp"))
    sender_section = jnp.arange(total, dtype=jnp.int32) // n
    counted = sender_section <= lax.axis_index("section")
    depth = jnp.sum(jnp.where(counted[:, None, None], scores, 0.0), axis=(0, 1))
    depth = depth.reshape(micro, queries)

    table_rows = prior_table.shape[0]
    first_row = lax.axis_index("dp") * table_rows
    own = first_row + jnp.arange(table_rows, dtype=jnp.int32)
    owner_mask = (seq_rows[None, :] == own[:, None]).astype(F32)
    result = prior_table + jnp.sum(owner_mask[:, :, None] * depth[None], axis=1)
    return result[None]


def solution(mesh):
    return jax.shard_map(
        per_device,
        mesh=mesh,
        in_specs=(
            P("section", None, "dp", None),
            P("section", None, "dp", None),
            P("section", "dp", None),
            P("section", "dp", None),
            P("section", "dp", None),
            P("section", None, "dp", None),
            P(),
            P(),
            P("dp", None),
        ),
        out_specs=P("section", "dp", None),
        check_vma=False,
    )
```

time: 304 us -> 60 us (0.20)
  other arithmetic: 106 us -> 3.86 us
  blocking collectives: 98.4 us -> 0 us
  local copies, waits for them, and re-layouts: 64.7 us -> 2.97 us
  waiting for transfers between devices: 0.04 us -> 32.9 us
  between operations: 13.6 us -> 0.23 us
  matrix products: 6.96 us -> 2.51 us
  starting transfers between devices: 13.4 us -> 17.1 us
    unnamed x2 -> x0, other arithmetic: 103 us -> none
    psum x2 -> x0, blocking collectives: 94.1 us -> none  [the longest x1 64.6 us: per_device(): act_proj = lax.psum(act_part, 'dp').astype(jnp.bfloat16)]
    all_to_all x2 -> x4, waiting for transfers between devices: 0.01 us -> 32.9 us  [exchange(): return lax.all_to_all(pieces, axes, split_axis=0, concat_axis=0, tiled=True)]
    unnamed x26 -> x14, local copies, waits for them, and re-layouts: 28.3 us -> 1.12 us
    all_to_all x2 -> x0, local copies, waits for them, and re-layouts: 18.5 us -> none  [the longest x1 13.9 us: per_device(): lax.all_to_all(activations[0], 'dp', split_axis=2, concat_axis=1, tiled=T...]
    squeeze x2 -> x0, local copies, waits for them, and re-layouts: 16.6 us -> none  [the longest x1 11.6 us: per_device(): activations[0]]
    all_gather x1 -> x0, blocking collectives: 4.35 us -> none  [entering(): pieces = lax.all_gather(value, axis)]
    all_to_all x2 -> x4, starting transfers between devices: 13.4 us -> 17.1 us  [exchange(): return lax.all_to_all(pieces, axes, split_axis=0, concat_axis=0, tiled=True)]
  transfers between devices with their start and end apart: 3 -> 4, of which waited for: 0 -> 4; matrix products, arithmetic and copies ran while one was open for 46% -> 0% of each run, Pallas kernels for 0% -> 0%
where the time goes in v1:
time: 60 us; the launch traced here: 59.5 us
  waiting for transfers between devices  32.9 us (55%)
  starting transfers between devices  17.1 us (29%)
  other arithmetic  3.86 us (6%)
  local copies, waits for them, and re-layouts  2.97 us (5%)
  matrix products  2.51 us (4%)
    all_to_all x4, waiting for transfers between devices, exchange(): return lax.all_to_all(pieces, axes, split_axis=0, concat_axis=0, tiled=True)  32.9 us
    all_to_all x4, starting transfers between devices, exchange(): return lax.all_to_all(pieces, axes, split_axis=0, concat_axis=0, tiled=True)  17.1 us
    dot_general x1, matrix products, per_device(): jnp.einsum('ri,qij->qrj', grad_own, precond, preferred_element_type=F32)  1.84 us
    transpose x1, other arithmetic, per_device(): pieces = jnp.concatenate([activations[0].reshape(own_rows, n, hidden_shar...  1.77 us
  transfers between devices with their start and end apart: 4, of which 4 were waited for; matrix products, arithmetic and copies ran while one was open for 0% of the time, Pallas kernels for 0%

profile of v1, /device:TPU:0, one launch (start us, length us, event | category | flops | bytes accessed | tf_op | source)
XLA Modules:
  0.0 59.5 jit_solution(18063123244020226760)
XLA Ops:
  0.0 0.0 copy-start
  0.0 1.8 %maximum_bitcast_fusion.1 = bf16[16,4,1152]{2,1,0:T(4,128)(2,1)} fusion(bf16[4,16,256]{2,0,1:T(4,128)(2,1)} %bitcast.38, bf16[4,16,896]{2,0,1:T(4,128)(2,1)} %bitcast.35), kind=kLoop, calls=%fused_computation.15 | loop fusion | flops 294912 | bytes 294912 | tf_op jit(solution)/shard_map/transpose | solution.py:43
  1.8 0.0 copy-start.1
  1.8 7.5 %all-to-all-start = ((bf16[16,4,1152]{2,1,0:T(4,128)(2,1)}), bf16[16,4,1152]{2,1,0:T(4,128)(2,1)S(1)}, u32[]{:S(2)}, u32[]{:S(2)}) async-start(bf16[16,4,1152]{2,1,0:T(4,128)(2,1)} %maximum_bitcast_fusion.1), calls=%async_computation | async-start | bytes 294912 | tf_op jit(solution)/shard_map/all_to_all | solution.py:12
  9.3 8.1 %all-to-all-done = bf16[16,4,1152]{2,1,0:T(4,128)(2,1)S(1)} async-done(((bf16[16,4,1152]{2,1,0:T(4,128)(2,1)}), bf16[16,4,1152]{2,1,0:T(4,128)(2,1)S(1)}, u32[]{:S(2)}, u32[]{:S(2)}) %all-to-all-start) | async-done | bytes 147488 | tf_op jit(solution)/shard_map/all_to_all | solution.py:12
  17.5 0.0 copy-done
  17.5 0.5 fusion.4
  18.0 0.0 copy-start.5
  18.0 0.0 copy-start.4
  18.0 0.2 reshape.129
  18.2 0.1 copy.28
  18.3 0.0 copy-done.1
  18.3 0.2 convolution_convert_fusion
  18.5 0.0 copy-start.2
  18.5 0.2 reshape.130
  18.7 0.1 copy.29
  18.8 0.8 %maximum_bitcast_fusion = bf16[16,64,128]{2,1,0:T(8,128)(2,1)} fusion(bf16[64,16,64]{2,0,1:T(8,128)(2,1)S(1)} %copy.29, bf16[64,16,64]{2,0,1:T(8,128)(2,1)S(1)} %copy.28), kind=kLoop, calls=%fused_computation.13 | loop fusion | flops 524288 | bytes 524288 | tf_op jit(solution)/shard_map/transpose | solution.py:54
  19.6 3.5 %all-to-all-start.1 = ((bf16[16,64,128]{2,1,0:T(8,128)(2,1)}), bf16[16,64,128]{2,1,0:T(8,128)(2,1)S(1)}, u32[]{:S(2)}, u32[]{:S(2)}) async-start(bf16[16,64,128]{2,1,0:T(8,128)(2,1)} %maximum_bitcast_fusion), calls=%async_computation.1 | async-start | bytes 524288 | tf_op jit(solution)/shard_map/all_to_all | solution.py:12
  23.2 0.0 copy-done.5
  23.2 0.1 convert_divide_fusion.1
  23.3 0.0 copy-done.4
  23.3 0.1 compare_convert_fusion
  23.3 9.8 %all-to-all-done.1 = bf16[16,64,128]{2,1,0:T(8,128)(2,1)S(1)} async-done(((bf16[16,64,128]{2,1,0:T(8,128)(2,1)}), bf16[16,64,128]{2,1,0:T(8,128)(2,1)S(1)}, u32[]{:S(2)}, u32[]{:S(2)}) %all-to-all-start.1) | async-done | bytes 262176 | tf_op jit(solution)/shard_map/all_to_all | solution.py:12
  33.2 0.9 %reshape.134 = bf16[16,2,2048]{2,1,0:T(2,128)(2,1)} reshape(bf16[16,64,64]{2,1,0:T(8,128)(2,1)S(1)} %broadcast_in_dim.35) | data formatting | bytes 262144
  34.1 3.5 %all-to-all-start.2 = ((bf16[16,2,2048]{2,1,0:T(2,128)(2,1)}), bf16[16,2,2048]{2,1,0:T(2,128)(2,1)S(1)}, u32[]{:S(2)}, u32[]{:S(2)}) async-start(bf16[16,2,2048]{2,1,0:T(2,128)(2,1)} %reshape.134), calls=%async_computation.2 | async-start | bytes 262144 | tf_op jit(solution)/shard_map/all_to_all | solution.py:12
  37.6 0.1 fusion.19
  37.7 0.0 copy-done.2
  37.8 7.8 %all-to-all-done.2 = bf16[16,2,2048]{2,1,0:T(2,128)(2,1)S(1)} async-done(((bf16[16,2,2048]{2,1,0:T(2,128)(2,1)}), bf16[16,2,2048]{2,1,0:T(2,128)(2,1)S(1)}, u32[]{:S(2)}, u32[]{:S(2)}) %all-to-all-start.2) | async-done | bytes 131104 | tf_op jit(solution)/shard_map/all_to_all | solution.py:12
  45.5 0.2 reshape.135
  45.8 0.3 copy.30
  46.1 0.2 reshape.132
  46.3 0.0 copy-start.3
  46.3 1.8 %fusion.1 = f32[8,64]{1,0:T(8,128)S(1)} fusion(bf16[1,8,64,1024]{3,2,1,0:T(8,128)(2,1)} %param.14, f32[64,1024]{1,0:T(8,128)S(1)} %reshape.132, f32[64,1024]{1,0:T(8,128)S(1)} %add_bitcast_fusion, bf16[64,128]{1,0:T(8,128)(2,1)S(1)} %convert_reduce_fusion, pred[64]{0:T(512)(128)(4,1)S(1)} %fusion.19), kind=kOutput, calls=%fused_computation.3 | convolution fusion | flops 69733888 | bytes 1591360 | tf_op jit(solution)/shard_map/ri,qij->qrj/dot_general | solution.py:69
  48.1 0.1 multiply_reduce_fusion.1
  48.2 0.1 broadcast_in_dim.36
  48.3 0.6 %broadcast_in_dim.58 = f32[32,1,32]{2,1,0:T(1,128)} broadcast(f32[32]{0:T(128)S(1)} %broadcast_in_dim.36), dimensions={2} | broadcast | bytes 4224 | tf_op jit(solution)/shard_map/broadcast_in_dim | solution.py:75
  48.9 2.6 %all-to-all-start.3 = ((f32[32,1,32]{2,1,0:T(1,128)}), f32[32,1,32]{2,1,0:T(1,128)S(1)}, u32[]{:S(2)}, u32[]{:S(2)}) async-start(f32[32,1,32]{2,1,0:T(1,128)} %broadcast_in_dim.58), calls=%async_computation.3 | async-start | bytes 32768 | tf_op jit(solution)/shard_map/all_to_all | solution.py:12
  51.5 7.2 %all-to-all-done.3 = f32[32,1,32]{2,1,0:T(1,128)S(1)} async-done(((f32[32,1,32]{2,1,0:T(1,128)}), f32[32,1,32]{2,1,0:T(1,128)S(1)}, u32[]{:S(2)}, u32[]{:S(2)}) %all-to-all-start.3) | async-done | bytes 4128 | tf_op jit(solution)/shard_map/all_to_all | solution.py:12
  58.6 0.1 broadcast_select_fusion
  58.8 0.1 mul.46
  58.9 0.1 multiply_reduce_fusion
  58.9 0.0 copy-done.3
  58.9 0.6 %add_bitcast_fusion.1 = f32[1,8,8]{2,1,0:T(8,128)} fusion(f32[8,8]{1,0:T(8,128)S(1)} %copy-done.3, f32[8,8]{1,0:T(8,128)S(1)} %multiply_reduce_fusion), kind=kLoop, calls=%fused_computation.27 | loop fusion | flops 64 | bytes 768 | tf_op jit(solution)/shard_map/broadcast_in_dim | solution.py:87
  (10 shorter events, 0.2 us)
Async XLA Ops:
  0.0 17.5 %copy-start = (bf16[1,896,1024]{2,1,0:T(8,128)(2,1)S(1)}, bf16[1,896,1024]{2,1,0:T(8,128)(2,1)}, u32[]{:S(2)}) copy-start(bf16[1,896,1024]{2,1,0:T(8,128)(2,1)} %param.11) | copy-start | bytes 5505028
  1.8 16.5 %copy-start.1 = (bf16[1,256,1024]{2,1,0:T(8,128)(2,1)S(1)}, bf16[1,256,1024]{2,1,0:T(8,128)(2,1)}, u32[]{:S(2)}) copy-start(bf16[1,256,1024]{2,1,0:T(8,128)(2,1)} %param.12) | copy-start | bytes 1572868
  1.8 15.7 %all-to-all-start = ((bf16[16,4,1152]{2,1,0:T(4,128)(2,1)}), bf16[16,4,1152]{2,1,0:T(4,128)(2,1)S(1)}, u32[]{:S(2)}, u32[]{:S(2)}) async-start(bf16[16,4,1152]{2,1,0:T(4,128)(2,1)} %maximum_bitcast_fusion.1), calls=%async_computation | async-start | bytes 294912 | tf_op jit(solution)/shard_map/all_to_all | solution.py:12
  18.0 5.2 %copy-start.5 = (s32[4]{0:T(128)S(1)}, s32[4]{0:T(128)}, u32[]{:S(2)}) copy-start(s32[4]{0:T(128)} %param.15) | copy-start | bytes 52
  18.0 5.3 %copy-start.4 = (s32[4]{0:T(128)S(1)}, s32[4]{0:T(128)}, u32[]{:S(2)}) copy-start(s32[4]{0:T(128)} %param.16) | copy-start | bytes 52
  18.5 19.2 %copy-start.2 = (f32[1,64,1024]{2,1,0:T(8,128)S(1)}, f32[1,64,1024]{2,1,0:T(8,128)}, u32[]{:S(2)}) copy-start(f32[1,64,1024]{2,1,0:T(8,128)} %param.13) | copy-start | bytes 786436
  19.6 13.5 %all-to-all-start.1 = ((bf16[16,64,128]{2,1,0:T(8,128)(2,1)}), bf16[16,64,128]{2,1,0:T(8,128)(2,1)S(1)}, u32[]{:S(2)}, u32[]{:S(2)}) async-start(bf16[16,64,128]{2,1,0:T(8,128)(2,1)} %maximum_bitcast_fusion), calls=%async_computation.1 | async-start | bytes 524288 | tf_op jit(solution)/shard_map/all_to_all | solution.py:12
  34.1 11.4 %all-to-all-start.2 = ((bf16[16,2,2048]{2,1,0:T(2,128)(2,1)}), bf16[16,2,2048]{2,1,0:T(2,128)(2,1)S(1)}, u32[]{:S(2)}, u32[]{:S(2)}) async-start(bf16[16,2,2048]{2,1,0:T(2,128)(2,1)} %reshape.134), calls=%async_computation.2 | async-start | bytes 262144 | tf_op jit(solution)/shard_map/all_to_all | solution.py:12
  46.3 12.7 %copy-start.3 = (f32[8,8]{1,0:T(8,128)S(1)}, f32[8,8]{1,0:T(8,128)}, u32[]{:S(2)}) copy-start(f32[8,8]{1,0:T(8,128)} %param.17) | copy-start | bytes 772
  48.9 9.7 %all-to-all-start.3 = ((f32[32,1,32]{2,1,0:T(1,128)}), f32[32,1,32]{2,1,0:T(1,128)S(1)}, u32[]{:S(2)}, u32[]{:S(2)}) async-start(f32[32,1,32]{2,1,0:T(1,128)} %broadcast_in_dim.58), calls=%async_computation.3 | async-start | bytes 32768 | tf_op jit(solution)/shard_map/all_to_all | solution.py:12

commit v2 on v1

--- a/solution.py
+++ b/solution.py
@@ -1,18 +1,258 @@
+import functools
+
 import jax
 import jax.numpy as jnp
 from jax import lax
+from jax.experimental import pallas as pl
+from jax.experimental.pallas import tpu as pltpu
 from jax.sharding import PartitionSpec as P
 
 DAMPING = 0.01
 F32 = jnp.float32
 BF16 = jnp.bfloat16
+LANES = 128
+VMEM = pl.BlockSpec(memory_space=pltpu.VMEM)
 
 
 def exchange(pieces, axes):
     return lax.all_to_all(pieces, axes, split_axis=0, concat_axis=0, tiled=True)
 
 
-def per_device(
+def call(body, out_shapes, *operands):
+    many = isinstance(out_shapes, (list, tuple))
+    return pl.pallas_call(
+        body,
+        out_shape=out_shapes,
+        in_specs=[VMEM] * len(operands),
+        out_specs=[VMEM] * len(out_shapes) if many else VMEM,
+        compiler_params=pltpu.CompilerParams(vmem_limit_bytes=16 << 20),
+    )(*operands)
+
+
+def place(peer, extra, rank):
+    across = rank // LANES
+    return pl.ds(peer // across * extra, extra), pl.ds(peer % across * LANES, LANES)
+
+
+def prep_kernel(lengths_ref, *refs):
+    eigen_hbm, query_hbm, grads_hbm, basis_hbm, kept_ref, precond_ref, weight_ref = refs[:7]
+    query_ref, eigen_ref, grads_ref, sems = refs[7:]
+    depth, rank = basis_hbm.shape
+    copies = [
+        pltpu.make_async_copy(source, target, sems.at[index])
+        for index, (source, target) in enumerate(
+            (
+                (eigen_hbm, eigen_ref),
+                (query_hbm, query_ref),
+                (grads_hbm, grads_ref),
+                (basis_hbm, kept_ref.at[:depth]),
+            )
+        )
+    ]
+    for copy in copies:
+        copy.start()
+    shape = weight_ref.shape
+    micro = lengths_ref.shape[1]
+    row = lax.broadcasted_iota(jnp.int32, shape, 0)
+    slot, member = row // micro, row % micro
+    length = jnp.zeros(shape, jnp.int32)
+    for index in range(micro):
+        length = jnp.where(member == index, lengths_ref[:, index : index + 1], length)
+    weight_ref[...] = jnp.where(slot < length, 1.0 / length.astype(F32), 0.0)
+    copies[0].wait()
+    copies[1].wait()
+    damped = eigen_ref[...] + DAMPING
+    for query in range(query_ref.shape[0]):
+        precond_ref[query] = (query_ref[query].astype(F32) / damped).astype(BF16)
+    copies[2].wait()
+    own_rows, features = grads_ref.shape
+    extra = 2 * own_rows
+    tail = kept_ref.at[depth:]
+    for peer in range(features // (2 * LANES)):
+        first = peer * 2 * LANES
+        left = grads_ref[:, first : first + LANES]
+        right = grads_ref[:, first + LANES : first + 2 * LANES]
+        tail[place(peer, extra, rank)] = jnp.concatenate([left, right], axis=0)
+    copies[3].wait()
+
+
+def act_kernel(rows_ref, kept_ref, out_ref):
+    peers, own_rows, share = rows_ref.shape
+    acts = rows_ref[...].reshape(peers * own_rows, share)
+    part = jnp.dot(acts, kept_ref[:share], preferred_element_type=F32).astype(BF16)
+    rank = part.shape[1]
+    blocks = rank // LANES
+    height = part.shape[0] * blocks // peers
+    for peer in range(peers):
+        group, block = peer // blocks, peer % blocks
+        out_ref[peer, :height] = part[
+            group * height : (group + 1) * height, block * LANES : (block + 1) * LANES
+        ]
+        out_ref[peer, height:] = kept_ref.at[share:][place(peer, 2 * own_rows, rank)]
+
+
+def halves(top, bottom, low):
+    return (
+        jnp.where(low, top, pltpu.roll(bottom, LANES // 2, 1)),
+        jnp.where(low, pltpu.roll(top, LANES // 2, 1), bottom),
+    )
+
+
+def grad_kernel(height, got_ref, basis_ref, out_ref):
+    peers = got_ref.shape[0]
+    total = got_ref[0, :height].astype(F32)
+    for peer in range(1, peers):
+        total += got_ref[peer, :height].astype(F32)
+    total = total.astype(BF16)
+    upper = lax.broadcasted_iota(jnp.int32, (8, LANES), 0) < 4
+    left, right = [], []
+    for pair in range(peers // 2):
+        one = got_ref[2 * pair, height:].astype(F32)
+        two = got_ref[2 * pair + 1, height:].astype(F32)
+        left.append(jnp.where(upper, one, pltpu.roll(two, 4, 0)))
+        right.append(jnp.where(upper, pltpu.roll(one, 4, 0), two))
+    grads = jnp.concatenate(
+        [jnp.concatenate(left, axis=0), jnp.concatenate(right, axis=0)], axis=1
+    ).astype(BF16)
+    part = jnp.dot(grads, basis_ref[...], preferred_element_type=F32)
+    half = part.shape[0] // 2
+    low = lax.broadcasted_iota(jnp.int32, (half, LANES), 1) < LANES // 2
+    for block in range(peers // 2):
+        at = block * LANES
+        one, two = halves(part[:half, at : at + LANES], part[half:, at : at + LANES], low)
+        for peer, piece in ((2 * block, one), (2 * block + 1, two)):
+            out_ref[peer, :height] = total
+            out_ref[peer, height:] = piece.astype(BF16)
+
+
+def score_kernel(height, got_ref, precond_ref, weight_ref, *refs):
+    out_ref = refs[-1]
+    peers = got_ref.shape[0]
+    queries, share, rank = precond_ref.shape
+    rows = weight_ref.shape[0]
+    blocks = rank // LANES
+    packed = got_ref[0, height:].astype(F32)
+    for peer in range(1, peers):
+        packed += got_ref[peer, height:].astype(F32)
+    grads = jnp.concatenate(
+        [packed[:, :share], pltpu.roll(packed, share, 1)[:, :share]], axis=0
+    ).astype(BF16)
+    lane = lax.broadcasted_iota(jnp.int32, (8, LANES), 1)
+    member = lax.broadcasted_iota(jnp.int32, (8, LANES), 0)
+    held = jnp.zeros((8, LANES), F32)
+    for query in range(queries):
+        turned = jnp.dot(grads, precond_ref[query], preferred_element_type=F32)
+        both = jnp.zeros((8, LANES), F32)
+        for group in range(rows // height):
+            top = group * height
+            acc = jnp.zeros((height, LANES), F32)
+            for block in range(blocks):
+                piece = turned[top : top + height, block * LANES : (block + 1) * LANES]
+                acc += piece * got_ref[group * blocks + block, :height].astype(F32)
+            acc *= weight_ref[top : top + height]
+            for first in range(0, height, 8):
+                both += acc[first : first + 8]
+        value = jnp.sum(both + pltpu.roll(both, 4, 0), axis=1, keepdims=True)
+        held = jnp.where(lane == member * queries + query, value, held)
+    held = jnp.where(member < 4, held, 0.0)
+    line = jnp.broadcast_to(jnp.sum(held, axis=0, keepdims=True), held.shape)
+    for first in range(0, out_ref.shape[0], 8):
+        out_ref[first : first + 8] = line
+
+
+def table_kernel(per_section, queries, got_ref, rows_ref, prior_ref, out_ref):
+    sender = lax.broadcasted_iota(jnp.int32, got_ref.shape, 0) // per_section
+    counted = sender <= lax.axis_index("section")
+    depth = jnp.sum(jnp.where(counted, got_ref[...], 0.0), axis=0, keepdims=True)
+    shape = prior_ref.shape
+    own = lax.axis_index("dp") * shape[0] + lax.broadcasted_iota(jnp.int32, shape, 0)
+    table = prior_ref[...]
+    for member in range(rows_ref.shape[1]):
+        first = member * queries
+        scores = jnp.broadcast_to(depth[:, first : first + queries], shape)
+        table += jnp.where(rows_ref[:, member : member + 1] == own, scores, 0.0)
+    out_ref[0] = table
+
+
+def packed_path(
+    activations,
+    out_grads,
+    basis_in,
+    basis_out,
+    eigen_values,
+    query_proj,
+    lengths,
+    seq_rows,
+    prior_table,
+):
+    n, sections = lax.axis_size("dp"), lax.axis_size("section")
+    micro, own_slots, hidden = activations.shape[1:]
+    features = out_grads.shape[3]
+    own_rows = micro * own_slots
+    rows = n * own_rows
+    rank = basis_in.shape[2]
+    queries = query_proj.shape[1]
+    height = rows * rank // (n * LANES)
+    extra = own_rows * features // (n * LANES)
+
+    lengths, seq_rows = lengths[None], seq_rows[None]
+    grads = out_grads[0].reshape(own_rows, features)
+
+    pieces = activations[0].reshape(own_rows, n, hidden // n).transpose(1, 0, 2)
+    got = exchange(pieces, "dp")
+    sources = (eigen_values[0], query_proj[0], grads, basis_in[0])
+    kept, precond, weight = pl.pallas_call(
+        prep_kernel,
+        out_shape=[
+            jax.ShapeDtypeStruct((hidden // n + n * extra * LANES // rank, rank), BF16),
+            jax.ShapeDtypeStruct(query_proj.shape[1:], BF16),
+            jax.ShapeDtypeStruct((rows, LANES), F32),
+        ],
+        in_specs=[VMEM] + [pl.BlockSpec(memory_space=pltpu.HBM)] * len(sources),
+        out_specs=[VMEM] * 3,
+        scratch_shapes=[
+            pltpu.VMEM(query_proj.shape[1:], BF16),
+            pltpu.VMEM(eigen_values.shape[1:], F32),
+            pltpu.VMEM((own_rows, features), BF16),
+            pltpu.SemaphoreType.DMA((len(sources),)),
+        ],
+        compiler_params=pltpu.CompilerParams(vmem_limit_bytes=16 << 20),
+    )(lengths, *(pltpu.with_memory_space_constraint(array, pltpu.HBM) for array in sources))
+    parts = call(
+        act_kernel,
+        jax.ShapeDtypeStruct((n, height + extra, LANES), BF16),
+        got,
+        kept,
+    )
+    parts = exchange(parts, "dp")
+    parts = call(
+        functools.partial(grad_kernel, height),
+        jax.ShapeDtypeStruct((n, 2 * height, LANES), BF16),
+        parts,
+        basis_out[0],
+    )
+    parts = exchange(parts, "dp")
+    total = n * sections
+    spread = call(
+        functools.partial(score_kernel, height),
+        jax.ShapeDtypeStruct((total, LANES), F32),
+        parts,
+        precond,
+        weight,
+        seq_rows,
+        prior_table,
+    )
+    scores = exchange(spread.reshape(total, 1, LANES), ("section", "dp")).reshape(total, LANES)
+    return call(
+        functools.partial(table_kernel, n, queries),
+        jax.ShapeDtypeStruct((1,) + prior_table.shape, F32),
+        scores,
+        seq_rows,
+        prior_table,
+    )
+
+
+def general_path(
     activations,
     out_grads,
     basis_in,
@@ -87,6 +327,26 @@
     return result[None]
 
 
+def per_device(*arrays):
+    activations, out_grads, basis_in, _, _, query_proj, _, _, prior_table = arrays
+    n = lax.axis_size("dp")
+    micro, own_slots, hidden = activations.shape[1:]
+    features = out_grads.shape[3]
+    rank = basis_in.shape[2]
+    queries = query_proj.shape[1]
+    packs = (
+        micro == 4
+        and own_slots == 1
+        and n % 8 == 0
+        and hidden % (n * LANES) == 0
+        and features == 2 * n * LANES
+        and 2 * rank == n * LANES
+        and micro * queries <= LANES
+        and prior_table.shape[0] % 8 == 0
+    )
+    return (packed_path if packs else general_path)(*arrays)
+
+
 def solution(mesh):
     return jax.shard_map(
         per_device,

time: 60 us -> 50.9 us (0.85)
  blocking collectives: 0 us -> 33.4 us
  waiting for transfers between devices: 32.9 us -> 4.4 us
  starting transfers between devices: 17.1 us -> 7.38 us
  Pallas kernels: 0 us -> 4.02 us
  other arithmetic: 3.86 us -> 0 us
  matrix products: 2.51 us -> 0 us
  local copies, waits for them, and re-layouts: 2.97 us -> 1.26 us
    all_to_all x0 -> x3, blocking collectives: none -> 33.4 us  [exchange(): return lax.all_to_all(pieces, axes, split_axis=0, concat_axis=0, tiled=True)]
    all_to_all x4 -> x1, waiting for transfers between devices: 32.9 us -> 4.4 us  [exchange(): return lax.all_to_all(pieces, axes, split_axis=0, concat_axis=0, tiled=True)]
    all_to_all x4 -> x1, starting transfers between devices: 17.1 us -> 7.38 us  [exchange(): return lax.all_to_all(pieces, axes, split_axis=0, concat_axis=0, tiled=True)]
    pallas_call x0 -> x5, Pallas kernels: none -> 4.02 us  [the longest x4 2.05 us: call(): pl.pallas_call(body, out_shape=out_shapes, in_specs=[VMEM] * len(operands...]
    transpose x2 -> x0, other arithmetic: 2.62 us -> none  [the longest x1 1.77 us: per_device(): pieces = jnp.concatenate([activations[0].reshape(own_rows, n, hidden_shar...]
    dot_general x3 -> x0, matrix products: 2.51 us -> none  [the longest x1 1.84 us: per_device(): jnp.einsum('ri,qij->qrj', grad_own, precond, preferred_element_type=F32)]
    broadcast_in_dim x3 -> x0, local copies, waits for them, and re-layouts: 0.74 us -> none  [the longest x2 0.7 us: per_device(): jnp.broadcast_to(partial.reshape(1, 1, micro * queries), (total, 1, micro...]
    unnamed x14 -> x12, local copies, waits for them, and re-layouts: 1.12 us -> 1.26 us
  transfers between devices with their start and end apart: 4 -> 1, of which waited for: 4 -> 1; matrix products, arithmetic and copies ran while one was open for 0% -> 0% of each run, Pallas kernels for 0% -> 4%
where the time goes in v2:
time: 50.9 us; the launch traced here: 50.6 us
  blocking collectives  33.4 us (66%)
  starting transfers between devices  7.38 us (14%)
  waiting for transfers between devices  4.4 us (9%)
  Pallas kernels  4.02 us (8%)
  local copies, waits for them, and re-layouts  1.26 us (2%)
    all_to_all x3, blocking collectives, exchange(): return lax.all_to_all(pieces, axes, split_axis=0, concat_axis=0, tiled=True)  33.4 us
    all_to_all x1, starting transfers between devices, exchange(): return lax.all_to_all(pieces, axes, split_axis=0, concat_axis=0, tiled=True)  7.38 us
    all_to_all x1, waiting for transfers between devices, exchange(): return lax.all_to_all(pieces, axes, split_axis=0, concat_axis=0, tiled=True)  4.4 us
    pallas_call x4, Pallas kernels, call(): pl.pallas_call(body, out_shape=out_shapes, in_specs=[VMEM] * len(operands...  2.05 us
    pallas_call x1, Pallas kernels, packed_path(): pl.pallas_call(prep_kernel, out_shape=[jax.ShapeDtypeStruct((hidden // n...  1.96 us
    unnamed x12, local copies, waits for them, and re-layouts  1.26 us
  transfers between devices with their start and end apart: 1, of which 1 were waited for; matrix products, arithmetic and copies ran while one was open for 0% of the time, Pallas kernels for 4%

profile of v2, /device:TPU:0, one launch (start us, length us, event | category | flops | bytes accessed | tf_op | source)
XLA Modules:
  0.0 50.6 jit_solution(2632913231614078973)
XLA Ops:
  0.0 7.4 %all-to-all-start = ((bf16[16,4,896]{2,1,0:T(4,128)(2,1)}), bf16[16,4,896]{2,1,0:T(4,128)(2,1)S(1)}, u32[]{:S(2)}, u32[]{:S(2)}) async-start(bf16[16,4,896]{2,1,0:T(4,128)(2,1)} %bitcast.23), calls=%async_computation | async-start | bytes 229376 | tf_op jit(solution)/shard_map/all_to_all | solution.py:18
  7.4 0.0 copy-start.5
  7.4 0.6 %copy-done.5 = s32[4]{0:T(128)S(1)} copy-done((s32[4]{0:T(128)S(1)}, s32[4]{0:T(128)}, u32[]{:S(2)}) %copy-start.5) | copy-done | bytes 40
  8.1 2.0 %shard_map.91 = (bf16[912,1024]{1,0:T(8,128)(2,1)S(1)}, bf16[8,64,1024]{2,1,0:T(8,128)(2,1)S(1)}, f32[64,128]{1,0:T(8,128)S(1)}) custom-call(s32[1,4]{1,0:T(1,128)S(1)} %bitcast.19, f32[64,1024]{1,0:T(8,128)} %bitcast.22, bf16[8,64,1024]{2,1,0:T(8,128)(2,1)} %bitcast.21, bf16[4,4096]{1,0:T(4,128)(2,1)} %bitcast.24, bf16[896,1024]{1,0:T(8,128)(2,1)} %bitcast.20), custom_call_target="tpu_custom_call" | custom-call | tf_op jit(solution)/shard_map/pallas_call | solution.py:204
  10.0 0.0 copy-start.1
  10.0 0.6 %copy-done.1 = f32[64,128]{1,0:T(8,128)} copy-done((f32[64,128]{1,0:T(8,128)}, f32[64,128]{1,0:T(8,128)S(1)}, u32[]{:S(2)}) %copy-start.1) | copy-done | bytes 32792
  10.6 0.0 copy-start
  10.6 4.4 %all-to-all-done.rows_ref = bf16[16,4,896]{2,1,0:T(4,128)(2,1)S(1)} async-done(((bf16[16,4,896]{2,1,0:T(4,128)(2,1)}), bf16[16,4,896]{2,1,0:T(4,128)(2,1)S(1)}, u32[]{:S(2)}, u32[]{:S(2)}) %all-to-all-start) | async-done | bytes 114720 | tf_op jit(solution)/shard_map/all_to_all | solution.py:18
  15.0 0.0 copy-start.2
  15.0 0.0 copy-start.3
  15.0 0.0 copy-start.4
  15.0 0.4 shard_map.92
  15.5 11.0 %all_to_all.20.got_ref = bf16[16,40,128]{2,1,0:T(8,128)(2,1)S(1)} all-to-all(bf16[16,40,128]{2,1,0:T(8,128)(2,1)S(1)} %shard_map.92), channel_id=1, replica_groups=mesh['section'=2,'dp'=16] {'dp'}, dimensions={0} | all-to-all | bytes 327680 | tf_op jit(solution)/shard_map/all_to_all | solution.py:18
  26.5 0.0 copy-done
  26.5 0.3 shard_map.93
  26.8 12.6 %all_to_all.21.got_ref = bf16[16,64,128]{2,1,0:T(8,128)(2,1)S(1)} all-to-all(bf16[16,64,128]{2,1,0:T(8,128)(2,1)S(1)} %shard_map.93), channel_id=1, replica_groups=mesh['section'=2,'dp'=16] {'dp'}, dimensions={0} | all-to-all | bytes 524288 | tf_op jit(solution)/shard_map/all_to_all | solution.py:18
  39.4 0.0 copy-done.2
  39.4 0.0 copy-done.3
  39.4 0.0 copy-done.4
  39.4 0.6 %shard_map.94 = f32[32,128]{1,0:T(8,128)S(1)} custom-call(bf16[16,64,128]{2,1,0:T(8,128)(2,1)S(1)} %all_to_all.21.got_ref, bf16[8,64,1024]{2,1,0:T(8,128)(2,1)S(1)} %get-tuple-element.9.precond_ref, f32[64,128]{1,0:T(8,128)S(1)} %copy-done.2, s32[1,4]{1,0:T(1,128)S(1)} %bitcast.17, f32[8,8]{1,0:T(8,128)S(1)} %copy-done.3), custom_call_target="tpu_custom_call" | custom-call | tf_op jit(solution)/shard_map/pallas_call | solution.py:23
  40.0 9.8 %all_to_all.22 = f32[32,1,128]{2,1,0:T(1,128)S(1)} all-to-all(f32[32,1,128]{2,1,0:T(1,128)S(1)} %bitcast.15), channel_id=1, replica_groups=mesh['section'=2,'dp'=16] {'section','dp'}, dimensions={0} | all-to-all | bytes 32768 | tf_op jit(solution)/shard_map/all_to_all | solution.py:18
  49.8 0.7 %shard_map.95 = f32[1,8,8]{2,1,0:T(8,128)} custom-call(f32[32,128]{1,0:T(8,128)S(1)} %bitcast.16, s32[1,4]{1,0:T(1,128)S(1)} %bitcast.18, f32[8,8]{1,0:T(8,128)S(1)} %copy-done.3), custom_call_target="tpu_custom_call" | custom-call | tf_op jit(solution)/shard_map/pallas_call | solution.py:23
Async XLA Ops:
  0.0 15.0 %all-to-all-start = ((bf16[16,4,896]{2,1,0:T(4,128)(2,1)}), bf16[16,4,896]{2,1,0:T(4,128)(2,1)S(1)}, u32[]{:S(2)}, u32[]{:S(2)}) async-start(bf16[16,4,896]{2,1,0:T(4,128)(2,1)} %bitcast.23), calls=%async_computation | async-start | bytes 229376 | tf_op jit(solution)/shard_map/all_to_all | solution.py:18
  7.4 0.7 %copy-start.5 = (s32[4]{0:T(128)S(1)}, s32[4]{0:T(128)}, u32[]{:S(2)}) copy-start(s32[4]{0:T(128)} %param.15) | copy-start | bytes 52
  10.0 0.6 %copy-start.1 = (f32[64,128]{1,0:T(8,128)}, f32[64,128]{1,0:T(8,128)S(1)}, u32[]{:S(2)}) copy-start(f32[64,128]{1,0:T(8,128)S(1)} %get-tuple-element.10.weight_ref) | copy-start | bytes 98308
  10.6 15.9 %copy-start = (bf16[1,256,1024]{2,1,0:T(8,128)(2,1)S(1)}, bf16[1,256,1024]{2,1,0:T(8,128)(2,1)}, u32[]{:S(2)}) copy-start(bf16[1,256,1024]{2,1,0:T(8,128)(2,1)} %param.12) | copy-start | bytes 1572868
  15.0 24.4 %copy-start.2 = (f32[64,128]{1,0:T(8,128)S(1)}, f32[64,128]{1,0:T(8,128)}, u32[]{:S(2)}) copy-start(f32[64,128]{1,0:T(8,128)} %copy-done.1) | copy-start | bytes 98308
  15.0 24.4 %copy-start.3 = (f32[8,8]{1,0:T(8,128)S(1)}, f32[8,8]{1,0:T(8,128)}, u32[]{:S(2)}) copy-start(f32[8,8]{1,0:T(8,128)} %prior_ref.1) | copy-start | bytes 772
  15.0 24.4 %copy-start.4 = (s32[4]{0:T(128)S(1)}, s32[4]{0:T(128)}, u32[]{:S(2)}) copy-start(s32[4]{0:T(128)} %param.16) | copy-start | bytes 52

commit v3 on v1

--- a/solution.py
+++ b/solution.py
@@ -1,18 +1,281 @@
+import functools
+
 import jax
 import jax.numpy as jnp
 from jax import lax
+from jax.experimental import pallas as pl
+from jax.experimental.pallas import tpu as pltpu
 from jax.sharding import PartitionSpec as P
+
 
 DAMPING = 0.01
 F32 = jnp.float32
 BF16 = jnp.bfloat16
+LANES = 128
+VMEM = pl.BlockSpec(memory_space=pltpu.VMEM)
 
 
 def exchange(pieces, axes):
     return lax.all_to_all(pieces, axes, split_axis=0, concat_axis=0, tiled=True)
 
 
-def per_device(
+def call(body, out_shapes, *operands):
+    many = isinstance(out_shapes, (list, tuple))
+    return pl.pallas_call(
+        body,
+        out_shape=out_shapes,
+        in_specs=[VMEM] * len(operands),
+        out_specs=[VMEM] * len(out_shapes) if many else VMEM,
+        compiler_params=pltpu.CompilerParams(vmem_limit_bytes=16 << 20),
+    )(*operands)
+
+
+def pack_kernel(acts_hbm, grads_hbm, basis_hbm, out_ref, basis_ref, acts_ref, grads_ref, sems):
+    copies = [
+        pltpu.make_async_copy(acts_hbm, acts_ref, sems.at[0]),
+        pltpu.make_async_copy(grads_hbm, grads_ref, sems.at[1]),
+        pltpu.make_async_copy(basis_hbm, basis_ref, sems.at[2]),
+    ]
+    for copy in copies:
+        copy.start()
+    peers = out_ref.shape[0]
+    hidden, features = acts_ref.shape[1] // peers, grads_ref.shape[1] // peers
+    copies[0].wait()
+    for peer in range(peers):
+        out_ref[peer, :, :hidden] = acts_ref[:, peer * hidden : (peer + 1) * hidden]
+    copies[1].wait()
+    for peer in range(peers):
+        out_ref[peer, :, hidden:] = grads_ref[:, peer * features : (peer + 1) * features]
+    copies[2].wait()
+
+
+def prep_kernel(lengths_ref, eigen_hbm, query_hbm, after_ref, *refs):
+    del after_ref
+    precond_ref, weight_ref, query_ref, eigen_ref, sems = refs
+    copies = [
+        pltpu.make_async_copy(eigen_hbm, eigen_ref, sems.at[0]),
+        pltpu.make_async_copy(query_hbm, query_ref, sems.at[1]),
+    ]
+    for copy in copies:
+        copy.start()
+    shape = weight_ref.shape
+    micro = lengths_ref.shape[1]
+    row = lax.axis_index("dp") % 2 * shape[0] + lax.broadcasted_iota(jnp.int32, shape, 0)
+    slot, member = row // micro, row % micro
+    length = jnp.zeros(shape, jnp.int32)
+    for index in range(micro):
+        length = jnp.where(member == index, lengths_ref[:, index : index + 1], length)
+    weight_ref[...] = jnp.where(slot < length, 1.0 / length.astype(F32), 0.0)
+    for copy in copies:
+        copy.wait()
+    damped = eigen_ref[...] + DAMPING
+    for query in range(query_ref.shape[0]):
+        precond_ref[query] = (query_ref[query].astype(F32) / damped).astype(BF16)
+
+
+def split_kernel(acts_ref, grads_ref, mine_ref, other_ref):
+    half, rank = mine_ref.shape[0], acts_ref.shape[1]
+    first = lax.axis_index("dp") % 2 == 0
+    for at, part_ref in ((0, acts_ref), (rank, grads_ref)):
+        top, bottom = part_ref[:half], part_ref[half:]
+        mine_ref[:, at : at + rank] = jnp.where(first, top, bottom)
+        other_ref[:, at : at + rank] = jnp.where(first, bottom, top)
+
+
+def pair_kernel(mine_ref, got_ref, keep_ref, send_ref):
+    total = mine_ref[...].astype(F32) + got_ref[...].astype(F32)
+    rank = total.shape[1] // 2
+    acts = total[:, :rank].astype(BF16)
+    keep_ref[:, :rank] = acts
+    send_ref[:, :rank] = acts
+    first = lax.axis_index("dp") // 2 % 2 == 0
+    for block in range(rank // (2 * LANES)):
+        at = rank + 2 * block * LANES
+        one, two = total[:, at : at + LANES], total[:, at + LANES : at + 2 * LANES]
+        to = rank + block * LANES
+        keep_ref[:, to : to + LANES] = jnp.where(first, one, two).astype(BF16)
+        send_ref[:, to : to + LANES] = jnp.where(first, two, one).astype(BF16)
+
+
+def plane_kernel(keep_ref, got_ref, out_ref):
+    total = (keep_ref[...].astype(F32) + got_ref[...].astype(F32)).astype(BF16)
+    peers, height, _ = out_ref.shape
+    rows = total.shape[0]
+    blocks = height // rows - 1
+    for peer in range(peers):
+        for block in range(blocks + 1):
+            at = (block if block < blocks else blocks + peer) * LANES
+            out_ref[peer, block * rows : (block + 1) * rows] = total[:, at : at + LANES]
+
+
+def score_kernel(got_ref, own_ref, swapped_ref, weight_ref, *refs):
+    out_ref = refs[-1]
+    peers = got_ref.shape[0]
+    queries, share, rank = own_ref.shape
+    rows = weight_ref.shape[0]
+    blocks = rank // LANES
+    total = got_ref[0].astype(F32)
+    for peer in range(1, peers):
+        total += got_ref[peer].astype(F32)
+    grads = total[blocks * rows :]
+    turned_lanes = pltpu.roll(grads, share, 1)
+    first = lax.axis_index("dp") % 2 == 0
+    own = jnp.where(first, grads, turned_lanes)[:, :share].astype(BF16)
+    swapped = jnp.where(first, turned_lanes, grads)[:, :share].astype(BF16)
+    lane = lax.broadcasted_iota(jnp.int32, (8, LANES), 1)
+    member = lax.broadcasted_iota(jnp.int32, (8, LANES), 0)
+    held = jnp.zeros((8, LANES), F32)
+    for query in range(queries):
+        turned = jnp.dot(own, own_ref[query], preferred_element_type=F32)
+        turned += jnp.dot(swapped, swapped_ref[query], preferred_element_type=F32)
+        acc = jnp.zeros((rows, LANES), F32)
+        for block in range(blocks):
+            acts = total[block * rows : (block + 1) * rows]
+            acc += turned[:, block * LANES : (block + 1) * LANES] * acts
+        acc *= weight_ref[...]
+        both = acc[:8]
+        for at in range(8, rows, 8):
+            both += acc[at : at + 8]
+        value = jnp.sum(both + pltpu.roll(both, 4, 0), axis=1, keepdims=True)
+        held = jnp.where(lane == member * queries + query, value, held)
+    held = jnp.where(member < 4, held, 0.0)
+    line = jnp.broadcast_to(jnp.sum(held, axis=0, keepdims=True), held.shape)
+    for at in range(0, out_ref.shape[0], 8):
+        out_ref[at : at + 8] = line
+
+
+def table_kernel(per_section, queries, got_ref, rows_ref, prior_ref, out_ref):
+    sender = lax.broadcasted_iota(jnp.int32, got_ref.shape, 0) // per_section
+    counted = sender <= lax.axis_index("section")
+    depth = jnp.sum(jnp.where(counted, got_ref[...], 0.0), axis=0, keepdims=True)
+    shape = prior_ref.shape
+    own = lax.axis_index("dp") * shape[0] + lax.broadcasted_iota(jnp.int32, shape, 0)
+    table = prior_ref[...]
+    for member in range(rows_ref.shape[1]):
+        first = member * queries
+        scores = jnp.broadcast_to(depth[:, first : first + queries], shape)
+        table += jnp.where(rows_ref[:, member : member + 1] == own, scores, 0.0)
+    out_ref[0] = table
+
+
+def packed_path(
+    activations,
+    out_grads,
+    basis_in,
+    basis_out,
+    eigen_values,
+    query_proj,
+    lengths,
+    seq_rows,
+    prior_table,
+):
+    n, sections = lax.axis_size("dp"), lax.axis_size("section")
+    micro, own_slots, hidden = activations.shape[1:]
+    features = out_grads.shape[3]
+    own_rows = micro * own_slots
+    half = n * own_rows // 2
+    rank = basis_in.shape[2]
+    width = (hidden + features) // n
+    lengths, seq_rows = lengths[None], seq_rows[None]
+    hbm = pl.BlockSpec(memory_space=pltpu.HBM)
+    params = pltpu.CompilerParams(vmem_limit_bytes=16 << 20)
+
+    def in_hbm(*arrays):
+        return [pltpu.with_memory_space_constraint(array, pltpu.HBM) for array in arrays]
+
+    def swap(value, bit):
+        return lax.ppermute(value, "dp", [(i, i ^ bit) for i in range(n)])
+
+    pieces, basis_out = pl.pallas_call(
+        pack_kernel,
+        out_shape=[
+            jax.ShapeDtypeStruct((n, own_rows, width), BF16),
+            jax.ShapeDtypeStruct(basis_out.shape[1:], BF16),
+        ],
+        in_specs=[hbm] * 3,
+        out_specs=[VMEM] * 2,
+        scratch_shapes=[
+            pltpu.VMEM((own_rows, hidden), BF16),
+            pltpu.VMEM((own_rows, features), BF16),
+            pltpu.SemaphoreType.DMA((3,)),
+        ],
+        compiler_params=params,
+    )(
+        *in_hbm(
+            activations[0].reshape(own_rows, hidden),
+            out_grads[0].reshape(own_rows, features),
+            basis_out[0],
+        )
+    )
+    got = exchange(pieces, "dp").reshape(2 * half, width)
+    share = hidden // n
+    mine, other = call(
+        split_kernel,
+        [jax.ShapeDtypeStruct((half, 2 * rank), BF16)] * 2,
+        jnp.dot(got[:, :share], basis_in[0], preferred_element_type=F32).astype(BF16),
+        jnp.dot(got[:, share:], basis_out, preferred_element_type=F32).astype(BF16),
+    )
+    keep, send = call(
+        pair_kernel,
+        [jax.ShapeDtypeStruct((half, rank + rank // 2), BF16)] * 2,
+        mine,
+        swap(other, 1),
+    )
+    beside = swap(send, 2)
+    prepare = pl.pallas_call(
+        prep_kernel,
+        out_shape=[
+            jax.ShapeDtypeStruct(query_proj.shape[1:], BF16),
+            jax.ShapeDtypeStruct((half, LANES), F32),
+        ],
+        in_specs=[VMEM, hbm, hbm, VMEM],
+        out_specs=[VMEM] * 2,
+        scratch_shapes=[
+            pltpu.VMEM(query_proj.shape[1:], BF16),
+            pltpu.VMEM(eigen_values.shape[1:], F32),
+            pltpu.SemaphoreType.DMA((2,)),
+        ],
+        compiler_params=params,
+    )
+    precond, weight = prepare(lengths, *in_hbm(eigen_values[0], query_proj[0]), keep)
+    swapped = swap(precond, 1)
+    planes = n // 4
+    parts = call(
+        plane_kernel,
+        jax.ShapeDtypeStruct((planes, half * (rank // LANES + 1), LANES), BF16),
+        keep,
+        beside,
+    )
+    parts = lax.all_to_all(
+        parts,
+        "dp",
+        split_axis=0,
+        concat_axis=0,
+        tiled=True,
+        axis_index_groups=[[4 * plane + spot for plane in range(planes)] for spot in range(4)],
+    )
+    total = n * sections
+    spread = call(
+        score_kernel,
+        jax.ShapeDtypeStruct((total, LANES), F32),
+        parts,
+        precond,
+        swapped,
+        weight,
+        seq_rows,
+        prior_table,
+    )
+    scores = exchange(spread.reshape(total, 1, LANES), ("section", "dp")).reshape(total, LANES)
+    return call(
+        functools.partial(table_kernel, n, query_proj.shape[1]),
+        jax.ShapeDtypeStruct((1,) + prior_table.shape, F32),
+        scores,
+        seq_rows,
+        prior_table,
+    )
+
+
+def general_path(
     activations,
     out_grads,
     basis_in,
@@ -87,6 +350,26 @@
     return result[None]
 
 
+def per_device(*arrays):
+    activations, out_grads, basis_in, _, _, query_proj, _, _, prior_table = arrays
+    n = lax.axis_size("dp")
+    micro, own_slots, hidden = activations.shape[1:]
+    features = out_grads.shape[3]
+    rank = basis_in.shape[2]
+    queries = query_proj.shape[1]
+    packs = (
+        micro == 4
+        and own_slots == 1
+        and n % 8 == 0
+        and hidden % (n * LANES) == 0
+        and features % (n * LANES) == 0
+        and 2 * rank == n * LANES
+        and micro * queries <= LANES
+        and prior_table.shape[0] % 8 == 0
+    )
+    return (packed_path if packs else general_path)(*arrays)
+
+
 def solution(mesh):
     return jax.shard_map(
         per_device,

time: 60 us -> 49 us (0.82)
  blocking collectives: 0 us -> 37 us
  waiting for transfers between devices: 32.9 us -> 6.4 us
  starting transfers between devices: 17.1 us -> 0.29 us
  Pallas kernels: 0 us -> 4.22 us
  other arithmetic: 3.86 us -> 0 us
  local copies, waits for them, and re-layouts: 2.97 us -> 0.06 us
  matrix products: 2.51 us -> 0.66 us
    all_to_all x0 -> x3, blocking collectives: none -> 37 us  [the longest x2 25.1 us: exchange(): return lax.all_to_all(pieces, axes, split_axis=0, concat_axis=0, tiled=True)]
    all_to_all x4 -> x0, waiting for transfers between devices: 32.9 us -> none  [exchange(): return lax.all_to_all(pieces, axes, split_axis=0, concat_axis=0, tiled=True)]
    all_to_all x4 -> x0, starting transfers between devices: 17.1 us -> none  [exchange(): return lax.all_to_all(pieces, axes, split_axis=0, concat_axis=0, tiled=True)]
    ppermute x0 -> x3, waiting for transfers between devices: none -> 6.4 us  [swap(): return lax.ppermute(value, 'dp', [(i, i ^ bit) for i in range(n)])]
    pallas_call x0 -> x7, Pallas kernels: none -> 4.22 us  [the longest x1 1.52 us: packed_path(): prepare(lengths, *in_hbm(eigen_values[0], query_proj[0]), keep)]
    transpose x2 -> x0, other arithmetic: 2.62 us -> none  [the longest x1 1.77 us: per_device(): pieces = jnp.concatenate([activations[0].reshape(own_rows, n, hidden_shar...]
    dot_general x3 -> x2, matrix products: 2.51 us -> 0.66 us  [the longest x1 0.45 us: packed_path(): jnp.dot(got[:, :share], basis_in[0], preferred_element_type=F32)]
    unnamed x14 -> x8, local copies, waits for them, and re-layouts: 1.12 us -> 0.02 us
  transfers between devices with their start and end apart: 4 -> 3, of which waited for: 4 -> 2; matrix products, arithmetic and copies ran while one was open for 0% -> 0% of each run, Pallas kernels for 0% -> 0%
where the time goes in v3:
time: 49 us; the launch traced here: 48.7 us
  blocking collectives  37 us (76%)
  waiting for transfers between devices  6.4 us (13%)
  Pallas kernels  4.22 us (9%)
  matrix products  0.66 us (1%)
    all_to_all x2, blocking collectives, exchange(): return lax.all_to_all(pieces, axes, split_axis=0, concat_axis=0, tiled=True)  25.1 us
    all_to_all x1, blocking collectives, packed_path(): lax.all_to_all(parts, 'dp', split_axis=0, concat_axis=0, tiled=True, axis...  11.9 us
    ppermute x3, waiting for transfers between devices, swap(): return lax.ppermute(value, 'dp', [(i, i ^ bit) for i in range(n)])  6.4 us
    pallas_call x1, Pallas kernels, packed_path(): prepare(lengths, *in_hbm(eigen_values[0], query_proj[0]), keep)  1.52 us
    pallas_call x5, Pallas kernels, call(): pl.pallas_call(body, out_shape=out_shapes, in_specs=[VMEM] * len(operands...  1.43 us
    pallas_call x1, Pallas kernels, packed_path(): pl.pallas_call(pack_kernel, out_shape=[jax.ShapeDtypeStruct((n, own_rows,...  1.27 us
  transfers between devices with their start and end apart: 3, of which 2 were waited for; matrix products, arithmetic and copies ran while one was open for 0% of the time, Pallas kernels for 0%

profile of v3, /device:TPU:0, one launch (start us, length us, event | category | flops | bytes accessed | tf_op | source)
XLA Modules:
  0.0 48.7 jit_solution(58234528584038263)
XLA Ops:
  0.0 0.0 copy-start
  0.0 1.3 %shard_map.91 = (bf16[16,4,1152]{2,1,0:T(4,128)(2,1)S(1)}, bf16[256,1024]{1,0:T(8,128)(2,1)S(1)}) custom-call(bf16[4,14336]{1,0:T(4,128)(2,1)} %bitcast.25, bf16[4,4096]{1,0:T(4,128)(2,1)} %bitcast.26, bf16[256,1024]{1,0:T(8,128)(2,1)} %bitcast.23), custom_call_target="tpu_custom_call" | custom-call | tf_op jit(solution)/shard_map/pallas_call | solution.py:189
  1.3 15.4 %all_to_all.15 = bf16[16,4,1152]{2,1,0:T(4,128)(2,1)S(1)} all-to-all(bf16[16,4,1152]{2,1,0:T(4,128)(2,1)S(1)} %get-tuple-element.13), channel_id=1, replica_groups=mesh['section'=2,'dp'=16] {'dp'}, dimensions={0} | all-to-all | bytes 294912 | tf_op jit(solution)/shard_map/all_to_all | solution.py:19
  16.6 0.0 copy-start.3
  16.7 0.2 convolution_convert_fusion.grads_ref
  16.9 0.0 copy-done
  16.9 0.5 fusion.2.acts_ref
  17.4 0.0 copy-start.1
  17.4 0.0 copy-start.2
  17.4 0.1 collective-permute-start
  17.5 1.3 %collective-permute-done.got_ref = bf16[32,2048]{1,0:T(8,128)(2,1)S(1)} collective-permute-done((bf16[32,2048]{1,0:T(8,128)(2,1)S(1)}, bf16[32,2048]{1,0:T(8,128)(2,1)S(1)}, u32[]{:S(2)}, u32[]{:S(2)}) %collective-permute-start) | collective-permute-done | bytes 131104 | tf_op jit(solution)/shard_map/ppermute | solution.py:187
  18.9 0.0 copy-done.3
  18.9 1.5 %shard_map.95 = (bf16[8,64,1024]{2,1,0:T(8,128)(2,1)S(1)}, f32[32,128]{1,0:T(8,128)S(1)}) custom-call(s32[1,4]{1,0:T(1,128)S(1)} %bitcast.21, f32[64,1024]{1,0:T(8,128)} %bitcast.24, bf16[8,64,1024]{2,1,0:T(8,128)(2,1)} %bitcast.22, bf16[32,1536]{1,0:T(8,128)(2,1)S(1)} %get-tuple-element.17.keep_ref.after_ref), custom_call_target="tpu_custom_call" | custom-call | tf_op jit(solution)/shard_map/pallas_call | solution.py:240
  20.4 0.2 collective-permute-start.2
  20.6 0.0 collective-permute-start.1
  20.6 5.1 %collective-permute-done.1.got_ref = bf16[32,1536]{1,0:T(8,128)(2,1)S(1)} collective-permute-done((bf16[32,1536]{1,0:T(8,128)(2,1)S(1)}, bf16[32,1536]{1,0:T(8,128)(2,1)S(1)}, u32[]{:S(2)}, u32[]{:S(2)}) %collective-permute-start.1) | collective-permute-done | bytes 98336 | tf_op jit(solution)/shard_map/ppermute | solution.py:187
  25.7 11.9 %all_to_all.16.got_ref = bf16[4,288,128]{2,1,0:T(8,128)(2,1)S(1)} all-to-all(bf16[4,288,128]{2,1,0:T(8,128)(2,1)S(1)} %shard_map.94), channel_id=1, replica_groups={{0,4,8,12},{1,5,9,13},{2,6,10,14},{3,7,11,15},{16,20,24,28},{17,21,25,2..., dimensions={0} | all-to-all | bytes 589824 | tf_op jit(solution)/shard_map/all_to_all | solution.py:249
  37.6 0.0 collective-permute-done.2.swapped_ref
  37.6 0.0 copy-done.1
  37.6 0.0 copy-done.2
  37.6 0.6 %shard_map.96 = f32[32,128]{1,0:T(8,128)S(1)} custom-call(bf16[4,288,128]{2,1,0:T(8,128)(2,1)S(1)} %all_to_all.16.got_ref, bf16[8,64,1024]{2,1,0:T(8,128)(2,1)S(1)} %get-tuple-element.19.own_ref, bf16[8,64,1024]{2,1,0:T(8,128)(2,1)S(1)} %collective-permute-done.2.swapped_ref, f32[32,128]{1,0:T(8,128)S(1)} %get-tuple-element.20.weight_ref, ...), custom_call_target="tpu_custom_call" | custom-call | tf_op jit(solution)/shard_map/pallas_call | solution.py:24
  38.2 9.8 %all_to_all.17 = f32[32,1,128]{2,1,0:T(1,128)S(1)} all-to-all(f32[32,1,128]{2,1,0:T(1,128)S(1)} %bitcast.17), channel_id=1, replica_groups=mesh['section'=2,'dp'=16] {'section','dp'}, dimensions={0} | all-to-all | bytes 32768 | tf_op jit(solution)/shard_map/all_to_all | solution.py:19
  48.0 0.7 %shard_map.97 = f32[1,8,8]{2,1,0:T(8,128)} custom-call(f32[32,128]{1,0:T(8,128)S(1)} %bitcast.18, s32[1,4]{1,0:T(1,128)S(1)} %bitcast.20, f32[8,8]{1,0:T(8,128)S(1)} %copy-done.1), custom_call_target="tpu_custom_call" | custom-call | tf_op jit(solution)/shard_map/pallas_call | solution.py:24
  (4 shorter events, 0.1 us)
Async XLA Ops:
  0.0 16.9 %copy-start = (bf16[1,896,1024]{2,1,0:T(8,128)(2,1)S(1)}, bf16[1,896,1024]{2,1,0:T(8,128)(2,1)}, u32[]{:S(2)}) copy-start(bf16[1,896,1024]{2,1,0:T(8,128)(2,1)} %param.11) | copy-start | bytes 5505028
  16.6 2.3 %copy-start.3 = (s32[4]{0:T(128)S(1)}, s32[4]{0:T(128)}, u32[]{:S(2)}) copy-start(s32[4]{0:T(128)} %param.15) | copy-start | bytes 52
  17.4 20.3 %copy-start.1 = (f32[8,8]{1,0:T(8,128)S(1)}, f32[8,8]{1,0:T(8,128)}, u32[]{:S(2)}) copy-start(f32[8,8]{1,0:T(8,128)} %prior_ref.1) | copy-start | bytes 772
  17.4 20.2 %copy-start.2 = (s32[4]{0:T(128)S(1)}, s32[4]{0:T(128)}, u32[]{:S(2)}) copy-start(s32[4]{0:T(128)} %param.16) | copy-start | bytes 52
  17.4 1.4 %collective-permute-start = (bf16[32,2048]{1,0:T(8,128)(2,1)S(1)}, bf16[32,2048]{1,0:T(8,128)(2,1)S(1)}, u32[]{:S(2)}, u32[]{:S(2)}) collective-permute-start(bf16[32,2048]{1,0:T(8,128)(2,1)S(1)} %get-tuple-element.16), channel_id=1, source_target_pairs={{0,1},{1,0},{2,3},{3,2},{4,5},{5,4},{6,7},{7,6},{8,9},{9,8},{10,11... | collective-permute-start | bytes 393224 | tf_op jit(solution)/shard_map/ppermute | solution.py:187
  20.4 17.2 %collective-permute-start.2 = (bf16[8,64,1024]{2,1,0:T(8,128)(2,1)S(1)}, bf16[8,64,1024]{2,1,0:T(8,128)(2,1)S(1)}, u32[]{:S(2)}, u32[]{:S(2)}) collective-permute-start(bf16[8,64,1024]{2,1,0:T(8,128)(2,1)S(1)} %get-tuple-element.19.own_ref), channel_id=1, source_target_pairs={{0,1},{1,0},{2,3},{3,2},{4,5},{5,4},{6,7},{7,6},{8,9},{9,8},{10,11... | collective-permute-start | bytes 3145736 | tf_op jit(solution)/shard_map/ppermute | solution.py:187
  20.6 5.1 %collective-permute-start.1 = (bf16[32,1536]{1,0:T(8,128)(2,1)S(1)}, bf16[32,1536]{1,0:T(8,128)(2,1)S(1)}, u32[]{:S(2)}, u32[]{:S(2)}) collective-permute-start(bf16[32,1536]{1,0:T(8,128)(2,1)S(1)} %get-tuple-element.18), channel_id=1, source_target_pairs={{0,2},{1,3},{2,0},{3,1},{4,6},{5,7},{6,4},{7,5},{8,10},{9,11},{10,... | collective-permute-start | bytes 294920 | tf_op jit(solution)/shard_map/ppermute | solution.py:187

commit v4 on v3

--- a/solution.py
+++ b/solution.py
@@ -79,59 +79,44 @@
     for at, part_ref in ((0, acts_ref), (rank, grads_ref)):
         top, bottom = part_ref[:half], part_ref[half:]
         mine_ref[:, at : at + rank] = jnp.where(first, top, bottom)
-        other_ref[:, at : at + rank] = jnp.where(first, bottom, top)
-
-
-def pair_kernel(mine_ref, got_ref, keep_ref, send_ref):
-    total = mine_ref[...].astype(F32) + got_ref[...].astype(F32)
-    rank = total.shape[1] // 2
-    acts = total[:, :rank].astype(BF16)
+        other_ref[:, at : at + rank] = jnp.where(first, bottom, top).astype(BF16)
+
+
+def fold_kernel(bit, mine_ref, got_ref, keep_ref, send_ref):
+    total = mine_ref[...] + got_ref[...].astype(F32)
+    width = keep_ref.shape[1]
+    rank = 2 * width - total.shape[1]
+    acts = total[:, :rank]
     keep_ref[:, :rank] = acts
-    send_ref[:, :rank] = acts
-    first = lax.axis_index("dp") // 2 % 2 == 0
-    for block in range(rank // (2 * LANES)):
-        at = rank + 2 * block * LANES
+    send_ref[:, :rank] = acts.astype(BF16)
+    first = lax.axis_index("dp") // bit % 2 == 0
+    for to in range(rank, width, LANES):
+        at = 2 * to - rank
         one, two = total[:, at : at + LANES], total[:, at + LANES : at + 2 * LANES]
-        to = rank + block * LANES
-        keep_ref[:, to : to + LANES] = jnp.where(first, one, two).astype(BF16)
+        keep_ref[:, to : to + LANES] = jnp.where(first, one, two)
         send_ref[:, to : to + LANES] = jnp.where(first, two, one).astype(BF16)
 
 
-def plane_kernel(keep_ref, got_ref, out_ref):
-    total = (keep_ref[...].astype(F32) + got_ref[...].astype(F32)).astype(BF16)
-    peers, height, _ = out_ref.shape
-    rows = total.shape[0]
-    blocks = height // rows - 1
-    for peer in range(peers):
-        for block in range(blocks + 1):
-            at = (block if block < blocks else blocks + peer) * LANES
-            out_ref[peer, block * rows : (block + 1) * rows] = total[:, at : at + LANES]
-
-
-def score_kernel(got_ref, own_ref, swapped_ref, weight_ref, *refs):
+def score_kernel(mine_ref, got_ref, own_ref, swapped_ref, weight_ref, *refs):
     out_ref = refs[-1]
-    peers = got_ref.shape[0]
     queries, share, rank = own_ref.shape
     rows = weight_ref.shape[0]
     blocks = rank // LANES
-    total = got_ref[0].astype(F32)
-    for peer in range(1, peers):
-        total += got_ref[peer].astype(F32)
-    grads = total[blocks * rows :]
+    total = mine_ref[...] + got_ref[...].astype(F32)
+    grads = total[:, rank:]
     turned_lanes = pltpu.roll(grads, share, 1)
     first = lax.axis_index("dp") % 2 == 0
-    own = jnp.where(first, grads, turned_lanes)[:, :share].astype(BF16)
-    swapped = jnp.where(first, turned_lanes, grads)[:, :share].astype(BF16)
+    sides = jnp.where(first, grads, turned_lanes).astype(BF16)
     lane = lax.broadcasted_iota(jnp.int32, (8, LANES), 1)
     member = lax.broadcasted_iota(jnp.int32, (8, LANES), 0)
     held = jnp.zeros((8, LANES), F32)
     for query in range(queries):
-        turned = jnp.dot(own, own_ref[query], preferred_element_type=F32)
-        turned += jnp.dot(swapped, swapped_ref[query], preferred_element_type=F32)
+        precond = jnp.concatenate([own_ref[query], swapped_ref[query]], axis=0)
+        turned = jnp.dot(sides, precond, preferred_element_type=F32)
         acc = jnp.zeros((rows, LANES), F32)
         for block in range(blocks):
-            acts = total[block * rows : (block + 1) * rows]
-            acc += turned[:, block * LANES : (block + 1) * LANES] * acts
+            at = block * LANES
+            acc += turned[:, at : at + LANES] * total[:, at : at + LANES]
         acc *= weight_ref[...]
         both = acc[:8]
         for at in range(8, rows, 8):
@@ -211,17 +196,25 @@
     share = hidden // n
     mine, other = call(
         split_kernel,
-        [jax.ShapeDtypeStruct((half, 2 * rank), BF16)] * 2,
-        jnp.dot(got[:, :share], basis_in[0], preferred_element_type=F32).astype(BF16),
-        jnp.dot(got[:, share:], basis_out, preferred_element_type=F32).astype(BF16),
-    )
-    keep, send = call(
-        pair_kernel,
-        [jax.ShapeDtypeStruct((half, rank + rank // 2), BF16)] * 2,
-        mine,
-        swap(other, 1),
-    )
-    beside = swap(send, 2)
+        [jax.ShapeDtypeStruct((half, 2 * rank), kind) for kind in (F32, BF16)],
+        jnp.dot(got[:, :share], basis_in[0], preferred_element_type=F32),
+        jnp.dot(got[:, share:], basis_out, preferred_element_type=F32),
+    )
+    keep, send, bit, prepared = mine, other, 1, None
+    while bit < n:
+        got = swap(send, bit)
+        if bit == 2:
+            prepared = keep
+        bit *= 2
+        if bit < n:
+            kinds = (F32, BF16)
+            width = rank + (keep.shape[1] - rank) // 2
+            keep, send = call(
+                functools.partial(fold_kernel, bit),
+                [jax.ShapeDtypeStruct((half, width), kind) for kind in kinds],
+                keep,
+                got,
+            )
     prepare = pl.pallas_call(
         prep_kernel,
         out_shape=[
@@ -237,28 +230,14 @@
         ],
         compiler_params=params,
     )
-    precond, weight = prepare(lengths, *in_hbm(eigen_values[0], query_proj[0]), keep)
+    precond, weight = prepare(lengths, *in_hbm(eigen_values[0], query_proj[0]), prepared)
     swapped = swap(precond, 1)
-    planes = n // 4
-    parts = call(
-        plane_kernel,
-        jax.ShapeDtypeStruct((planes, half * (rank // LANES + 1), LANES), BF16),
-        keep,
-        beside,
-    )
-    parts = lax.all_to_all(
-        parts,
-        "dp",
-        split_axis=0,
-        concat_axis=0,
-        tiled=True,
-        axis_index_groups=[[4 * plane + spot for plane in range(planes)] for spot in range(4)],
-    )
     total = n * sections
     spread = call(
         score_kernel,
         jax.ShapeDtypeStruct((total, LANES), F32),
-        parts,
+        keep,
+        got,
         precond,
         swapped,
         weight,
@@ -360,7 +339,8 @@
     packs = (
         micro == 4
         and own_slots == 1
-        and n % 8 == 0
+        and n & (n - 1) == 0
+        and n >= 8
         and hidden % (n * LANES) == 0
         and features % (n * LANES) == 0
         and 2 * rank == n * LANES

time: 49 us -> 47.2 us (0.963)
  blocking collectives: 37 us -> 25.2 us
  waiting for transfers between devices: 6.4 us -> 15.8 us
  starting transfers between devices: 0.29 us -> 0.89 us
    all_to_all x1 -> x0, blocking collectives: 11.9 us -> none  [packed_path(): lax.all_to_all(parts, 'dp', split_axis=0, concat_axis=0, tiled=True, axis...]
    ppermute x3 -> x5, waiting for transfers between devices: 6.4 us -> 15.8 us  [swap(): return lax.ppermute(value, 'dp', [(i, i ^ bit) for i in range(n)])]
    ppermute x3 -> x5, starting transfers between devices: 0.29 us -> 0.89 us  [swap(): return lax.ppermute(value, 'dp', [(i, i ^ bit) for i in range(n)])]
    pallas_call x5 -> x6, Pallas kernels: 1.43 us -> 1.42 us  [call(): pl.pallas_call(body, out_shape=out_shapes, in_specs=[VMEM] * len(operands...]
  transfers between devices with their start and end apart: 3 -> 5, of which waited for: 2 -> 4; matrix products, arithmetic and copies ran while one was open for 0% -> 0% of each run, Pallas kernels for 0% -> 0%
where the time goes in v4:
time: 47.2 us; the launch traced here: 47 us
  blocking collectives  25.2 us (53%)
  waiting for transfers between devices  15.8 us (33%)
  Pallas kernels  4.22 us (9%)
  starting transfers between devices  0.89 us (2%)
  matrix products  0.64 us (1%)
    all_to_all x2, blocking collectives, exchange(): return lax.all_to_all(pieces, axes, split_axis=0, concat_axis=0, tiled=True)  25.2 us
    ppermute x5, waiting for transfers between devices, swap(): return lax.ppermute(value, 'dp', [(i, i ^ bit) for i in range(n)])  15.8 us
    pallas_call x1, Pallas kernels, packed_path(): prepare(lengths, *in_hbm(eigen_values[0], query_proj[0]), prepared)  1.52 us
    pallas_call x6, Pallas kernels, call(): pl.pallas_call(body, out_shape=out_shapes, in_specs=[VMEM] * len(operands...  1.42 us
    pallas_call x1, Pallas kernels, packed_path(): pl.pallas_call(pack_kernel, out_shape=[jax.ShapeDtypeStruct((n, own_rows,...  1.27 us
  transfers between devices with their start and end apart: 5, of which 4 were waited for; matrix products, arithmetic and copies ran while one was open for 0% of the time, Pallas kernels for 0%

profile of v4, /device:TPU:0, one launch (start us, length us, event | category | flops | bytes accessed | tf_op | source)
XLA Modules:
  0.0 47.0 jit_solution(5646247455613587949)
XLA Ops:
  0.0 0.0 copy-start
  0.0 1.3 %shard_map.91 = (bf16[16,4,1152]{2,1,0:T(4,128)(2,1)S(1)}, bf16[256,1024]{1,0:T(8,128)(2,1)S(1)}) custom-call(bf16[4,14336]{1,0:T(4,128)(2,1)} %bitcast.23, bf16[4,4096]{1,0:T(4,128)(2,1)} %bitcast.24, bf16[256,1024]{1,0:T(8,128)(2,1)} %bitcast.21), custom_call_target="tpu_custom_call" | custom-call | tf_op jit(solution)/shard_map/pallas_call | solution.py:174
  1.3 15.4 %all_to_all.10 = bf16[16,4,1152]{2,1,0:T(4,128)(2,1)S(1)} all-to-all(bf16[16,4,1152]{2,1,0:T(4,128)(2,1)S(1)} %get-tuple-element.17), channel_id=1, replica_groups=mesh['section'=2,'dp'=16] {'dp'}, dimensions={0} | all-to-all | bytes 294912 | tf_op jit(solution)/shard_map/all_to_all | solution.py:19
  16.7 0.0 copy-start.3
  16.7 0.2 fusion.3.grads_ref
  16.9 0.0 copy-done
  16.9 0.4 fusion.acts_ref
  17.4 0.0 copy-start.1
  17.4 0.0 copy-start.2
  17.4 0.1 shard_map.92
  17.4 0.1 collective-permute-start
  17.5 1.3 %collective-permute-done.got_ref = bf16[32,2048]{1,0:T(8,128)(2,1)S(1)} collective-permute-done((bf16[32,2048]{1,0:T(8,128)(2,1)S(1)}, bf16[32,2048]{1,0:T(8,128)(2,1)S(1)}, u32[]{:S(2)}, u32[]{:S(2)}) %collective-permute-start) | collective-permute-done | bytes 131104 | tf_op jit(solution)/shard_map/ppermute | solution.py:172
  18.9 0.0 copy-done.3
  18.9 1.5 %shard_map.96 = (bf16[8,64,1024]{2,1,0:T(8,128)(2,1)S(1)}, f32[32,128]{1,0:T(8,128)S(1)}) custom-call(s32[1,4]{1,0:T(1,128)S(1)} %bitcast.19, f32[64,1024]{1,0:T(8,128)} %bitcast.22, bf16[8,64,1024]{2,1,0:T(8,128)(2,1)} %bitcast.20, f32[32,1536]{1,0:T(8,128)S(1)} %get-tuple-element.21.mine_ref.after_ref), custom_call_target="tpu_custom_call" | custom-call | tf_op jit(solution)/shard_map/pallas_call | solution.py:233
  20.4 0.2 collective-permute-start.4
  20.6 0.0 collective-permute-start.1
  20.6 5.1 %collective-permute-done.1.got_ref = bf16[32,1536]{1,0:T(8,128)(2,1)S(1)} collective-permute-done((bf16[32,1536]{1,0:T(8,128)(2,1)S(1)}, bf16[32,1536]{1,0:T(8,128)(2,1)S(1)}, u32[]{:S(2)}, u32[]{:S(2)}) %collective-permute-start.1) | collective-permute-done | bytes 98336 | tf_op jit(solution)/shard_map/ppermute | solution.py:172
  25.7 0.1 collective-permute-start.2
  25.8 4.4 %collective-permute-done.2.got_ref = bf16[32,1280]{1,0:T(8,128)(2,1)S(1)} collective-permute-done((bf16[32,1280]{1,0:T(8,128)(2,1)S(1)}, bf16[32,1280]{1,0:T(8,128)(2,1)S(1)}, u32[]{:S(2)}, u32[]{:S(2)}) %collective-permute-start.2) | collective-permute-done | bytes 81952 | tf_op jit(solution)/shard_map/ppermute | solution.py:172
  30.3 0.5 %collective-permute-start.3 = (bf16[32,1152]{1,0:T(8,128)(2,1)S(1)}, bf16[32,1152]{1,0:T(8,128)(2,1)S(1)}, u32[]{:S(2)}, u32[]{:S(2)}) collective-permute-start(bf16[32,1152]{1,0:T(8,128)(2,1)S(1)} %get-tuple-element.26), channel_id=1, source_target_pairs={{0,8},{1,9},{2,10},{3,11},{4,12},{5,13},{6,14},{7,15},{8,0},{9,1},... | collective-permute-start | bytes 221192 | tf_op jit(solution)/shard_map/ppermute | solution.py:172
  30.8 5.0 %collective-permute-done.3.got_ref = bf16[32,1152]{1,0:T(8,128)(2,1)S(1)} collective-permute-done((bf16[32,1152]{1,0:T(8,128)(2,1)S(1)}, bf16[32,1152]{1,0:T(8,128)(2,1)S(1)}, u32[]{:S(2)}, u32[]{:S(2)}) %collective-permute-start.3) | collective-permute-done | bytes 73760 | tf_op jit(solution)/shard_map/ppermute | solution.py:172
  35.8 0.0 collective-permute-done.4.swapped_ref
  35.8 0.0 copy-done.1
  35.8 0.0 copy-done.2
  35.8 0.6 %shard_map.97 = f32[32,128]{1,0:T(8,128)S(1)} custom-call(f32[32,1152]{1,0:T(8,128)S(1)} %get-tuple-element.25.mine_ref, bf16[32,1152]{1,0:T(8,128)(2,1)S(1)} %collective-permute-done.3.got_ref, bf16[8,64,1024]{2,1,0:T(8,128)(2,1)S(1)} %get-tuple-element.27.own_ref, bf16[8,64,1024]{2,1,0:T(8,128)(2,1)S(1)} %collective-permute-done.4.swapped_ref, ...), custom_call_target="tpu_custom_call" | custom-call | tf_op jit(solution)/shard_map/pallas_call | solution.py:24
  36.4 9.9 %all_to_all.11 = f32[32,1,128]{2,1,0:T(1,128)S(1)} all-to-all(f32[32,1,128]{2,1,0:T(1,128)S(1)} %bitcast.15), channel_id=1, replica_groups=mesh['section'=2,'dp'=16] {'section','dp'}, dimensions={0} | all-to-all | bytes 32768 | tf_op jit(solution)/shard_map/all_to_all | solution.py:19
  46.3 0.7 %shard_map.98 = f32[1,8,8]{2,1,0:T(8,128)} custom-call(f32[32,128]{1,0:T(8,128)S(1)} %bitcast.16, s32[1,4]{1,0:T(1,128)S(1)} %bitcast.18, f32[8,8]{1,0:T(8,128)S(1)} %copy-done.1), custom_call_target="tpu_custom_call" | custom-call | tf_op jit(solution)/shard_map/pallas_call | solution.py:24
  (4 shorter events, 0.1 us)
Async XLA Ops:
  0.0 16.9 %copy-start = (bf16[1,896,1024]{2,1,0:T(8,128)(2,1)S(1)}, bf16[1,896,1024]{2,1,0:T(8,128)(2,1)}, u32[]{:S(2)}) copy-start(bf16[1,896,1024]{2,1,0:T(8,128)(2,1)} %param.11) | copy-start | bytes 5505028
  16.7 2.2 %copy-start.3 = (s32[4]{0:T(128)S(1)}, s32[4]{0:T(128)}, u32[]{:S(2)}) copy-start(s32[4]{0:T(128)} %param.15) | copy-start | bytes 52
  17.4 18.5 %copy-start.1 = (f32[8,8]{1,0:T(8,128)S(1)}, f32[8,8]{1,0:T(8,128)}, u32[]{:S(2)}) copy-start(f32[8,8]{1,0:T(8,128)} %prior_ref.1) | copy-start | bytes 772
  17.4 18.5 %copy-start.2 = (s32[4]{0:T(128)S(1)}, s32[4]{0:T(128)}, u32[]{:S(2)}) copy-start(s32[4]{0:T(128)} %param.16) | copy-start | bytes 52
  17.4 1.4 %collective-permute-start = (bf16[32,2048]{1,0:T(8,128)(2,1)S(1)}, bf16[32,2048]{1,0:T(8,128)(2,1)S(1)}, u32[]{:S(2)}, u32[]{:S(2)}) collective-permute-start(bf16[32,2048]{1,0:T(8,128)(2,1)S(1)} %get-tuple-element.20), channel_id=1, source_target_pairs={{0,1},{1,0},{2,3},{3,2},{4,5},{5,4},{6,7},{7,6},{8,9},{9,8},{10,11... | collective-permute-start | bytes 393224 | tf_op jit(solution)/shard_map/ppermute | solution.py:172
  20.4 15.4 %collective-permute-start.4 = (bf16[8,64,1024]{2,1,0:T(8,128)(2,1)S(1)}, bf16[8,64,1024]{2,1,0:T(8,128)(2,1)S(1)}, u32[]{:S(2)}, u32[]{:S(2)}) collective-permute-start(bf16[8,64,1024]{2,1,0:T(8,128)(2,1)S(1)} %get-tuple-element.27.own_ref), channel_id=1, source_target_pairs={{0,1},{1,0},{2,3},{3,2},{4,5},{5,4},{6,7},{7,6},{8,9},{9,8},{10,11... | collective-permute-start | bytes 3145736 | tf_op jit(solution)/shard_map/ppermute | solution.py:172
  20.6 5.1 %collective-permute-start.1 = (bf16[32,1536]{1,0:T(8,128)(2,1)S(1)}, bf16[32,1536]{1,0:T(8,128)(2,1)S(1)}, u32[]{:S(2)}, u32[]{:S(2)}) collective-permute-start(bf16[32,1536]{1,0:T(8,128)(2,1)S(1)} %get-tuple-element.22), channel_id=1, source_target_pairs={{0,2},{1,3},{2,0},{3,1},{4,6},{5,7},{6,4},{7,5},{8,10},{9,11},{10,... | collective-permute-start | bytes 294920 | tf_op jit(solution)/shard_map/ppermute | solution.py:172
  25.7 4.5 %collective-permute-start.2 = (bf16[32,1280]{1,0:T(8,128)(2,1)S(1)}, bf16[32,1280]{1,0:T(8,128)(2,1)S(1)}, u32[]{:S(2)}, u32[]{:S(2)}) collective-permute-start(bf16[32,1280]{1,0:T(8,128)(2,1)S(1)} %get-tuple-element.24), channel_id=1, source_target_pairs={{0,4},{1,5},{2,6},{3,7},{4,0},{5,1},{6,2},{7,3},{8,12},{9,13},{10,... | collective-permute-start | bytes 245768 | tf_op jit(solution)/shard_map/ppermute | solution.py:172
  30.3 5.5 %collective-permute-start.3 = (bf16[32,1152]{1,0:T(8,128)(2,1)S(1)}, bf16[32,1152]{1,0:T(8,128)(2,1)S(1)}, u32[]{:S(2)}, u32[]{:S(2)}) collective-permute-start(bf16[32,1152]{1,0:T(8,128)(2,1)S(1)} %get-tuple-element.26), channel_id=1, source_target_pairs={{0,8},{1,9},{2,10},{3,11},{4,12},{5,13},{6,14},{7,15},{8,0},{9,1},... | collective-permute-start | bytes 221192 | tf_op jit(solution)/shard_map/ppermute | solution.py:172

commit v5 on v4

--- a/solution.py
+++ b/solution.py
@@ -82,19 +82,29 @@
         other_ref[:, at : at + rank] = jnp.where(first, bottom, top).astype(BF16)
 
 
-def fold_kernel(bit, mine_ref, got_ref, keep_ref, send_ref):
-    total = mine_ref[...] + got_ref[...].astype(F32)
-    width = keep_ref.shape[1]
-    rank = 2 * width - total.shape[1]
-    acts = total[:, :rank]
-    keep_ref[:, :rank] = acts
-    send_ref[:, :rank] = acts.astype(BF16)
-    first = lax.axis_index("dp") // bit % 2 == 0
-    for to in range(rank, width, LANES):
-        at = 2 * to - rank
-        one, two = total[:, at : at + LANES], total[:, at + LANES : at + 2 * LANES]
-        keep_ref[:, to : to + LANES] = jnp.where(first, one, two)
-        send_ref[:, to : to + LANES] = jnp.where(first, two, one).astype(BF16)
+def fold_kernel(bits, count, *refs):
+    total = refs[0][...]
+    for got_ref in refs[1:count]:
+        total += got_ref[...].astype(F32)
+    outs = refs[count:]
+    ways = len(outs)
+    width = outs[0].shape[1]
+    blocks = (total.shape[1] - width) // LANES // (ways - 1)
+    rank = width - blocks * LANES
+    low = [lax.axis_index("dp") // bit % 2 == 0 for bit in bits]
+    for offset, out_ref in enumerate(outs):
+        out_ref[:, :rank] = total[:, :rank].astype(out_ref.dtype)
+        for block in range(blocks):
+            at = rank + block * ways * LANES
+            left = [total[:, at + way * LANES : at + (way + 1) * LANES] for way in range(ways)]
+            for place, mine in enumerate(low):
+                flip = offset >> place & 1
+                left = [
+                    jnp.where(mine, left[pair + flip], left[pair + 1 - flip])
+                    for pair in range(0, len(left), 2)
+                ]
+            to = rank + block * LANES
+            out_ref[:, to : to + LANES] = left[0].astype(out_ref.dtype)
 
 
 def score_kernel(mine_ref, got_ref, own_ref, swapped_ref, weight_ref, *refs):
@@ -200,21 +210,23 @@
         jnp.dot(got[:, :share], basis_in[0], preferred_element_type=F32),
         jnp.dot(got[:, share:], basis_out, preferred_element_type=F32),
     )
-    keep, send, bit, prepared = mine, other, 1, None
-    while bit < n:
-        got = swap(send, bit)
-        if bit == 2:
+    keep, gots = mine, [swap(other, 1)]
+    prepared = None
+    for bits in [(2, 4)] + [(1 << place,) for place in range(3, n.bit_length() - 1)]:
+        ways = 1 << len(bits)
+        width = rank + (keep.shape[1] - rank) // ways
+        keep, *sends = call(
+            functools.partial(fold_kernel, bits, 1 + len(gots)),
+            [jax.ShapeDtypeStruct((half, width), kind) for kind in [F32] + [BF16] * (ways - 1)],
+            keep,
+            *gots,
+        )
+        if prepared is None:
             prepared = keep
-        bit *= 2
-        if bit < n:
-            kinds = (F32, BF16)
-            width = rank + (keep.shape[1] - rank) // 2
-            keep, send = call(
-                functools.partial(fold_kernel, bit),
-                [jax.ShapeDtypeStruct((half, width), kind) for kind in kinds],
-                keep,
-                got,
-            )
+        gots = []
+        for offset, send in enumerate(sends, 1):
+            gots.append(swap(send, offset * bits[0]))
+    (got,) = gots
     prepare = pl.pallas_call(
         prep_kernel,
         out_shape=[
@@ -340,7 +352,7 @@
         micro == 4
         and own_slots == 1
         and n & (n - 1) == 0
-        and n >= 8
+        and n >= 16
         and hidden % (n * LANES) == 0
         and features % (n * LANES) == 0
         and 2 * rank == n * LANES

time: 47.2 us -> 45.4 us (0.962)
  waiting for transfers between devices: 15.8 us -> 10.8 us
  starting transfers between devices: 0.89 us -> 4.3 us
    ppermute x5 -> x6, waiting for transfers between devices: 15.8 us -> 10.8 us  [swap(): return lax.ppermute(value, 'dp', [(i, i ^ bit) for i in range(n)])]
    ppermute x5 -> x6, starting transfers between devices: 0.89 us -> 4.3 us  [swap(): return lax.ppermute(value, 'dp', [(i, i ^ bit) for i in range(n)])]
    pallas_call x6 -> x5, Pallas kernels: 1.42 us -> 1.43 us  [call(): pl.pallas_call(body, out_shape=out_shapes, in_specs=[VMEM] * len(operands...]
  transfers between devices with their start and end apart: 5 -> 6, of which waited for: 4 -> 5; matrix products, arithmetic and copies ran while one was open for 0% -> 0% of each run, Pallas kernels for 0% -> 0%
where the time goes in v5:
time: 45.4 us; the launch traced here: 45.1 us
  blocking collectives  25 us (55%)
  waiting for transfers between devices  10.8 us (24%)
  starting transfers between devices  4.3 us (9%)
  Pallas kernels  4.22 us (9%)
  matrix products  0.64 us (1%)
    all_to_all x2, blocking collectives, exchange(): return lax.all_to_all(pieces, axes, split_axis=0, concat_axis=0, tiled=True)  25 us
    ppermute x6, waiting for transfers between devices, swap(): return lax.ppermute(value, 'dp', [(i, i ^ bit) for i in range(n)])  10.8 us
    ppermute x6, starting transfers between devices, swap(): return lax.ppermute(value, 'dp', [(i, i ^ bit) for i in range(n)])  4.3 us
    pallas_call x1, Pallas kernels, packed_path(): prepare(lengths, *in_hbm(eigen_values[0], query_proj[0]), prepared)  1.52 us
    pallas_call x5, Pallas kernels, call(): pl.pallas_call(body, out_shape=out_shapes, in_specs=[VMEM] * len(operands...  1.43 us
    pallas_call x1, Pallas kernels, packed_path(): pl.pallas_call(pack_kernel, out_shape=[jax.ShapeDtypeStruct((n, own_rows,...  1.27 us
  transfers between devices with their start and end apart: 6, of which 5 were waited for; matrix products, arithmetic and copies ran while one was open for 0% of the time, Pallas kernels for 0%

profile of v5, /device:TPU:0, one launch (start us, length us, event | category | flops | bytes accessed | tf_op | source)
XLA Modules:
  0.0 45.1 jit_solution(16413818860909451415)
XLA Ops:
  0.0 0.0 copy-start
  0.0 1.3 %shard_map.91 = (bf16[16,4,1152]{2,1,0:T(4,128)(2,1)S(1)}, bf16[256,1024]{1,0:T(8,128)(2,1)S(1)}) custom-call(bf16[4,14336]{1,0:T(4,128)(2,1)} %bitcast.23, bf16[4,4096]{1,0:T(4,128)(2,1)} %bitcast.24, bf16[256,1024]{1,0:T(8,128)(2,1)} %bitcast.21), custom_call_target="tpu_custom_call" | custom-call | tf_op jit(solution)/shard_map/pallas_call | solution.py:184
  1.3 15.4 %all_to_all.10 = bf16[16,4,1152]{2,1,0:T(4,128)(2,1)S(1)} all-to-all(bf16[16,4,1152]{2,1,0:T(4,128)(2,1)S(1)} %get-tuple-element.17), channel_id=1, replica_groups=mesh['section'=2,'dp'=16] {'dp'}, dimensions={0} | all-to-all | bytes 294912 | tf_op jit(solution)/shard_map/all_to_all | solution.py:19
  16.7 0.0 copy-start.3
  16.7 0.2 fusion.3.grads_ref
  16.9 0.0 copy-done
  16.9 0.4 fusion.acts_ref
  17.4 0.0 copy-start.1
  17.4 0.0 copy-start.2
  17.4 0.1 shard_map.92
  17.4 0.1 collective-permute-start
  17.5 1.3 %collective-permute-done.refs_1_ = bf16[32,2048]{1,0:T(8,128)(2,1)S(1)} collective-permute-done((bf16[32,2048]{1,0:T(8,128)(2,1)S(1)}, bf16[32,2048]{1,0:T(8,128)(2,1)S(1)}, u32[]{:S(2)}, u32[]{:S(2)}) %collective-permute-start) | collective-permute-done | bytes 131104 | tf_op jit(solution)/shard_map/ppermute | solution.py:182
  18.9 0.0 copy-done.3
  18.9 1.5 %shard_map.95 = (bf16[8,64,1024]{2,1,0:T(8,128)(2,1)S(1)}, f32[32,128]{1,0:T(8,128)S(1)}) custom-call(s32[1,4]{1,0:T(1,128)S(1)} %bitcast.19, f32[64,1024]{1,0:T(8,128)} %bitcast.22, bf16[8,64,1024]{2,1,0:T(8,128)(2,1)} %bitcast.20, f32[32,1280]{1,0:T(8,128)S(1)} %get-tuple-element.21.refs_0_.after_ref), custom_call_target="tpu_custom_call" | custom-call | tf_op jit(solution)/shard_map/pallas_call | solution.py:245
  20.4 0.2 collective-permute-start.5
  20.7 0.0 collective-permute-start.1
  20.7 0.7 %collective-permute-start.2 = (bf16[32,1280]{1,0:T(8,128)(2,1)S(1)}, bf16[32,1280]{1,0:T(8,128)(2,1)S(1)}, u32[]{:S(2)}, u32[]{:S(2)}) collective-permute-start(bf16[32,1280]{1,0:T(8,128)(2,1)S(1)} %get-tuple-element.23), channel_id=1, source_target_pairs={{0,4},{1,5},{2,6},{3,7},{4,0},{5,1},{6,2},{7,3},{8,12},{9,13},{10,... | collective-permute-start | bytes 245768 | tf_op jit(solution)/shard_map/ppermute | solution.py:182
  21.3 2.8 %collective-permute-start.3 = (bf16[32,1280]{1,0:T(8,128)(2,1)S(1)}, bf16[32,1280]{1,0:T(8,128)(2,1)S(1)}, u32[]{:S(2)}, u32[]{:S(2)}) collective-permute-start(bf16[32,1280]{1,0:T(8,128)(2,1)S(1)} %get-tuple-element.24), channel_id=1, source_target_pairs={{0,6},{1,7},{2,4},{3,5},{4,2},{5,3},{6,0},{7,1},{8,14},{9,15},{10,... | collective-permute-start | bytes 245768 | tf_op jit(solution)/shard_map/ppermute | solution.py:182
  24.1 1.2 %collective-permute-done.1.refs_1_ = bf16[32,1280]{1,0:T(8,128)(2,1)S(1)} collective-permute-done((bf16[32,1280]{1,0:T(8,128)(2,1)S(1)}, bf16[32,1280]{1,0:T(8,128)(2,1)S(1)}, u32[]{:S(2)}, u32[]{:S(2)}) %collective-permute-start.1) | collective-permute-done | bytes 81952 | tf_op jit(solution)/shard_map/ppermute | solution.py:182
  25.4 0.6 %collective-permute-done.2.refs_2_ = bf16[32,1280]{1,0:T(8,128)(2,1)S(1)} collective-permute-done((bf16[32,1280]{1,0:T(8,128)(2,1)S(1)}, bf16[32,1280]{1,0:T(8,128)(2,1)S(1)}, u32[]{:S(2)}, u32[]{:S(2)}) %collective-permute-start.2) | collective-permute-done | bytes 81952 | tf_op jit(solution)/shard_map/ppermute | solution.py:182
  25.9 2.4 %collective-permute-done.3.refs_3_ = bf16[32,1280]{1,0:T(8,128)(2,1)S(1)} collective-permute-done((bf16[32,1280]{1,0:T(8,128)(2,1)S(1)}, bf16[32,1280]{1,0:T(8,128)(2,1)S(1)}, u32[]{:S(2)}, u32[]{:S(2)}) %collective-permute-start.3) | collective-permute-done | bytes 81952 | tf_op jit(solution)/shard_map/ppermute | solution.py:182
  28.3 0.5 %collective-permute-start.4 = (bf16[32,1152]{1,0:T(8,128)(2,1)S(1)}, bf16[32,1152]{1,0:T(8,128)(2,1)S(1)}, u32[]{:S(2)}, u32[]{:S(2)}) collective-permute-start(bf16[32,1152]{1,0:T(8,128)(2,1)S(1)} %get-tuple-element.26), channel_id=1, source_target_pairs={{0,8},{1,9},{2,10},{3,11},{4,12},{5,13},{6,14},{7,15},{8,0},{9,1},... | collective-permute-start | bytes 221192 | tf_op jit(solution)/shard_map/ppermute | solution.py:182
  28.9 5.3 %collective-permute-done.4.got_ref = bf16[32,1152]{1,0:T(8,128)(2,1)S(1)} collective-permute-done((bf16[32,1152]{1,0:T(8,128)(2,1)S(1)}, bf16[32,1152]{1,0:T(8,128)(2,1)S(1)}, u32[]{:S(2)}, u32[]{:S(2)}) %collective-permute-start.4) | collective-permute-done | bytes 73760 | tf_op jit(solution)/shard_map/ppermute | solution.py:182
  34.2 0.0 collective-permute-done.5.swapped_ref
  34.2 0.0 copy-done.1
  34.2 0.0 copy-done.2
  34.2 0.6 %shard_map.96 = f32[32,128]{1,0:T(8,128)S(1)} custom-call(f32[32,1152]{1,0:T(8,128)S(1)} %get-tuple-element.25.mine_ref, bf16[32,1152]{1,0:T(8,128)(2,1)S(1)} %collective-permute-done.4.got_ref, bf16[8,64,1024]{2,1,0:T(8,128)(2,1)S(1)} %get-tuple-element.27.own_ref, bf16[8,64,1024]{2,1,0:T(8,128)(2,1)S(1)} %collective-permute-done.5.swapped_ref, ...), custom_call_target="tpu_custom_call" | custom-call | tf_op jit(solution)/shard_map/pallas_call | solution.py:24
  34.7 9.7 %all_to_all.11 = f32[32,1,128]{2,1,0:T(1,128)S(1)} all-to-all(f32[32,1,128]{2,1,0:T(1,128)S(1)} %bitcast.15), channel_id=1, replica_groups=mesh['section'=2,'dp'=16] {'section','dp'}, dimensions={0} | all-to-all | bytes 32768 | tf_op jit(solution)/shard_map/all_to_all | solution.py:19
  44.4 0.7 %shard_map.97 = f32[1,8,8]{2,1,0:T(8,128)} custom-call(f32[32,128]{1,0:T(8,128)S(1)} %bitcast.16, s32[1,4]{1,0:T(1,128)S(1)} %bitcast.18, f32[8,8]{1,0:T(8,128)S(1)} %copy-done.1), custom_call_target="tpu_custom_call" | custom-call | tf_op jit(solution)/shard_map/pallas_call | solution.py:24
  (3 shorter events, 0.1 us)
Async XLA Ops:
  0.0 16.9 %copy-start = (bf16[1,896,1024]{2,1,0:T(8,128)(2,1)S(1)}, bf16[1,896,1024]{2,1,0:T(8,128)(2,1)}, u32[]{:S(2)}) copy-start(bf16[1,896,1024]{2,1,0:T(8,128)(2,1)} %param.11) | copy-start | bytes 5505028
  16.7 2.2 %copy-start.3 = (s32[4]{0:T(128)S(1)}, s32[4]{0:T(128)}, u32[]{:S(2)}) copy-start(s32[4]{0:T(128)} %param.15) | copy-start | bytes 52
  17.4 16.8 %copy-start.1 = (f32[8,8]{1,0:T(8,128)S(1)}, f32[8,8]{1,0:T(8,128)}, u32[]{:S(2)}) copy-start(f32[8,8]{1,0:T(8,128)} %prior_ref.1) | copy-start | bytes 772
  17.4 16.8 %copy-start.2 = (s32[4]{0:T(128)S(1)}, s32[4]{0:T(128)}, u32[]{:S(2)}) copy-start(s32[4]{0:T(128)} %param.16) | copy-start | bytes 52
  17.4 1.4 %collective-permute-start = (bf16[32,2048]{1,0:T(8,128)(2,1)S(1)}, bf16[32,2048]{1,0:T(8,128)(2,1)S(1)}, u32[]{:S(2)}, u32[]{:S(2)}) collective-permute-start(bf16[32,2048]{1,0:T(8,128)(2,1)S(1)} %get-tuple-element.20), channel_id=1, source_target_pairs={{0,1},{1,0},{2,3},{3,2},{4,5},{5,4},{6,7},{7,6},{8,9},{9,8},{10,11... | collective-permute-start | bytes 393224 | tf_op jit(solution)/shard_map/ppermute | solution.py:182
  20.4 13.7 %collective-permute-start.5 = (bf16[8,64,1024]{2,1,0:T(8,128)(2,1)S(1)}, bf16[8,64,1024]{2,1,0:T(8,128)(2,1)S(1)}, u32[]{:S(2)}, u32[]{:S(2)}) collective-permute-start(bf16[8,64,1024]{2,1,0:T(8,128)(2,1)S(1)} %get-tuple-element.27.own_ref), channel_id=1, source_target_pairs={{0,1},{1,0},{2,3},{3,2},{4,5},{5,4},{6,7},{7,6},{8,9},{9,8},{10,11... | collective-permute-start | bytes 3145736 | tf_op jit(solution)/shard_map/ppermute | solution.py:182
  20.7 4.7 %collective-permute-start.1 = (bf16[32,1280]{1,0:T(8,128)(2,1)S(1)}, bf16[32,1280]{1,0:T(8,128)(2,1)S(1)}, u32[]{:S(2)}, u32[]{:S(2)}) collective-permute-start(bf16[32,1280]{1,0:T(8,128)(2,1)S(1)} %get-tuple-element.22), channel_id=1, source_target_pairs={{0,2},{1,3},{2,0},{3,1},{4,6},{5,7},{6,4},{7,5},{8,10},{9,11},{10,... | collective-permute-start | bytes 245768 | tf_op jit(solution)/shard_map/ppermute | solution.py:182
  20.7 5.3 %collective-permute-start.2 = (bf16[32,1280]{1,0:T(8,128)(2,1)S(1)}, bf16[32,1280]{1,0:T(8,128)(2,1)S(1)}, u32[]{:S(2)}, u32[]{:S(2)}) collective-permute-start(bf16[32,1280]{1,0:T(8,128)(2,1)S(1)} %get-tuple-element.23), channel_id=1, source_target_pairs={{0,4},{1,5},{2,6},{3,7},{4,0},{5,1},{6,2},{7,3},{8,12},{9,13},{10,... | collective-permute-start | bytes 245768 | tf_op jit(solution)/shard_map/ppermute | solution.py:182
  21.3 7.0 %collective-permute-start.3 = (bf16[32,1280]{1,0:T(8,128)(2,1)S(1)}, bf16[32,1280]{1,0:T(8,128)(2,1)S(1)}, u32[]{:S(2)}, u32[]{:S(2)}) collective-permute-start(bf16[32,1280]{1,0:T(8,128)(2,1)S(1)} %get-tuple-element.24), channel_id=1, source_target_pairs={{0,6},{1,7},{2,4},{3,5},{4,2},{5,3},{6,0},{7,1},{8,14},{9,15},{10,... | collective-permute-start | bytes 245768 | tf_op jit(solution)/shard_map/ppermute | solution.py:182
  28.3 5.8 %collective-permute-start.4 = (bf16[32,1152]{1,0:T(8,128)(2,1)S(1)}, bf16[32,1152]{1,0:T(8,128)(2,1)S(1)}, u32[]{:S(2)}, u32[]{:S(2)}) collective-permute-start(bf16[32,1152]{1,0:T(8,128)(2,1)S(1)} %get-tuple-element.26), channel_id=1, source_target_pairs={{0,8},{1,9},{2,10},{3,11},{4,12},{5,13},{6,14},{7,15},{8,0},{9,1},... | collective-permute-start | bytes 221192 | tf_op jit(solution)/shard_map/ppermute | solution.py:182

commit v6 on v5

--- a/solution.py
+++ b/solution.py
@@ -30,14 +30,13 @@
     )(*operands)
 
 
-def pack_kernel(acts_hbm, grads_hbm, basis_hbm, out_ref, basis_ref, acts_ref, grads_ref, sems):
+def pack_kernel(acts_hbm, grads_hbm, out_ref, acts_ref, grads_ref, sems):
     copies = [
         pltpu.make_async_copy(acts_hbm, acts_ref, sems.at[0]),
         pltpu.make_async_copy(grads_hbm, grads_ref, sems.at[1]),
-        pltpu.make_async_copy(basis_hbm, basis_ref, sems.at[2]),
     ]
     for copy in copies:
-        copy.start()
+        copy.start(priority=1)
     peers = out_ref.shape[0]
     hidden, features = acts_ref.shape[1] // peers, grads_ref.shape[1] // peers
     copies[0].wait()
@@ -46,7 +45,6 @@
     copies[1].wait()
     for peer in range(peers):
         out_ref[peer, :, hidden:] = grads_ref[:, peer * features : (peer + 1) * features]
-    copies[2].wait()
 
 
 def prep_kernel(lengths_ref, eigen_hbm, query_hbm, after_ref, *refs):
@@ -73,11 +71,13 @@
         precond_ref[query] = (query_ref[query].astype(F32) / damped).astype(BF16)
 
 
-def split_kernel(acts_ref, grads_ref, mine_ref, other_ref):
+def split_kernel(acts_ref, rows_ref, basis_ref, mine_ref, other_ref):
     half, rank = mine_ref.shape[0], acts_ref.shape[1]
     first = lax.axis_index("dp") % 2 == 0
-    for at, part_ref in ((0, acts_ref), (rank, grads_ref)):
-        top, bottom = part_ref[:half], part_ref[half:]
+    rows = rows_ref[:, rows_ref.shape[1] - basis_ref.shape[0] :]
+    grads = jnp.dot(rows, basis_ref[...], preferred_element_type=F32)
+    for at, part in ((0, acts_ref[...]), (rank, grads)):
+        top, bottom = part[:half], part[half:]
         mine_ref[:, at : at + rank] = jnp.where(first, top, bottom)
         other_ref[:, at : at + rank] = jnp.where(first, bottom, top).astype(BF16)
 
@@ -181,25 +181,21 @@
     def swap(value, bit):
         return lax.ppermute(value, "dp", [(i, i ^ bit) for i in range(n)])
 
-    pieces, basis_out = pl.pallas_call(
+    pieces = pl.pallas_call(
         pack_kernel,
-        out_shape=[
-            jax.ShapeDtypeStruct((n, own_rows, width), BF16),
-            jax.ShapeDtypeStruct(basis_out.shape[1:], BF16),
-        ],
-        in_specs=[hbm] * 3,
-        out_specs=[VMEM] * 2,
+        out_shape=jax.ShapeDtypeStruct((n, own_rows, width), BF16),
+        in_specs=[hbm] * 2,
+        out_specs=VMEM,
         scratch_shapes=[
             pltpu.VMEM((own_rows, hidden), BF16),
             pltpu.VMEM((own_rows, features), BF16),
-            pltpu.SemaphoreType.DMA((3,)),
+            pltpu.SemaphoreType.DMA((2,)),
         ],
         compiler_params=params,
     )(
         *in_hbm(
             activations[0].reshape(own_rows, hidden),
             out_grads[0].reshape(own_rows, features),
-            basis_out[0],
         )
     )
     got = exchange(pieces, "dp").reshape(2 * half, width)
@@ -208,7 +204,8 @@
         split_kernel,
         [jax.ShapeDtypeStruct((half, 2 * rank), kind) for kind in (F32, BF16)],
         jnp.dot(got[:, :share], basis_in[0], preferred_element_type=F32),
-        jnp.dot(got[:, share:], basis_out, preferred_element_type=F32),
+        got,
+        basis_out[0],
     )
     keep, gots = mine, [swap(other, 1)]
     prepared = None

time: 45.4 us -> 45.1 us (level)
  no operation moved by 1% of the time
where the time goes in v6:
time: 45.1 us; the launch traced here: 44.9 us
  blocking collectives  25 us (55%)
  waiting for transfers between devices  10.8 us (24%)
  starting transfers between devices  4.3 us (10%)
  Pallas kernels  4.18 us (9%)
    all_to_all x2, blocking collectives, exchange(): return lax.all_to_all(pieces, axes, split_axis=0, concat_axis=0, tiled=True)  25 us
    ppermute x6, waiting for transfers between devices, swap(): return lax.ppermute(value, 'dp', [(i, i ^ bit) for i in range(n)])  10.8 us
    ppermute x6, starting transfers between devices, swap(): return lax.ppermute(value, 'dp', [(i, i ^ bit) for i in range(n)])  4.3 us
    pallas_call x5, Pallas kernels, call(): pl.pallas_call(body, out_shape=out_shapes, in_specs=[VMEM] * len(operands...  1.58 us
    pallas_call x1, Pallas kernels, packed_path(): prepare(lengths, *in_hbm(eigen_values[0], query_proj[0]), prepared)  1.52 us
    pallas_call x1, Pallas kernels, packed_path(): pl.pallas_call(pack_kernel, out_shape=jax.ShapeDtypeStruct((n, own_rows,...  1.08 us
  transfers between devices with their start and end apart: 6, of which 5 were waited for; matrix products, arithmetic and copies ran while one was open for 0% of the time, Pallas kernels for 0%

profile of v6, /device:TPU:0, one launch (start us, length us, event | category | flops | bytes accessed | tf_op | source)
XLA Modules:
  0.0 44.9 jit_solution(7718251101293559317)
XLA Ops:
  0.0 0.0 copy-start
  0.0 0.0 copy-start.1
  0.0 1.1 %shard_map.91 = bf16[16,4,1152]{2,1,0:T(4,128)(2,1)S(1)} custom-call(bf16[4,14336]{1,0:T(4,128)(2,1)} %bitcast.22, bf16[4,4096]{1,0:T(4,128)(2,1)} %bitcast.23), custom_call_target="tpu_custom_call" | custom-call | tf_op jit(solution)/shard_map/pallas_call | solution.py:184
  1.1 15.4 %all_to_all.10 = bf16[16,4,1152]{2,1,0:T(4,128)(2,1)S(1)} all-to-all(bf16[16,4,1152]{2,1,0:T(4,128)(2,1)S(1)} %shard_map.91), channel_id=1, replica_groups=mesh['section'=2,'dp'=16] {'dp'}, dimensions={0} | all-to-all | bytes 294912 | tf_op jit(solution)/shard_map/all_to_all | solution.py:19
  16.5 0.0 copy-done
  16.5 0.0 copy-start.4
  16.5 0.4 fusion.acts_ref
  17.0 0.0 copy-start.2
  17.0 0.0 copy-start.3
  17.0 0.0 copy-done.1
  17.0 0.2 shard_map.92
  17.2 0.1 collective-permute-start
  17.3 1.3 %collective-permute-done.refs_1_ = bf16[32,2048]{1,0:T(8,128)(2,1)S(1)} collective-permute-done((bf16[32,2048]{1,0:T(8,128)(2,1)S(1)}, bf16[32,2048]{1,0:T(8,128)(2,1)S(1)}, u32[]{:S(2)}, u32[]{:S(2)}) %collective-permute-start) | collective-permute-done | bytes 131104 | tf_op jit(solution)/shard_map/ppermute | solution.py:182
  18.7 0.0 copy-done.4
  18.7 1.5 %shard_map.95 = (bf16[8,64,1024]{2,1,0:T(8,128)(2,1)S(1)}, f32[32,128]{1,0:T(8,128)S(1)}) custom-call(s32[1,4]{1,0:T(1,128)S(1)} %bitcast.19, f32[64,1024]{1,0:T(8,128)} %bitcast.21, bf16[8,64,1024]{2,1,0:T(8,128)(2,1)} %bitcast.20, f32[32,1280]{1,0:T(8,128)S(1)} %get-tuple-element.17.refs_0_.after_ref), custom_call_target="tpu_custom_call" | custom-call | tf_op jit(solution)/shard_map/pallas_call | solution.py:242
  20.2 0.2 collective-permute-start.5
  20.4 0.0 collective-permute-start.1
  20.4 0.7 %collective-permute-start.2 = (bf16[32,1280]{1,0:T(8,128)(2,1)S(1)}, bf16[32,1280]{1,0:T(8,128)(2,1)S(1)}, u32[]{:S(2)}, u32[]{:S(2)}) collective-permute-start(bf16[32,1280]{1,0:T(8,128)(2,1)S(1)} %get-tuple-element.19), channel_id=1, source_target_pairs={{0,4},{1,5},{2,6},{3,7},{4,0},{5,1},{6,2},{7,3},{8,12},{9,13},{10,... | collective-permute-start | bytes 245768 | tf_op jit(solution)/shard_map/ppermute | solution.py:182
  21.1 2.8 %collective-permute-start.3 = (bf16[32,1280]{1,0:T(8,128)(2,1)S(1)}, bf16[32,1280]{1,0:T(8,128)(2,1)S(1)}, u32[]{:S(2)}, u32[]{:S(2)}) collective-permute-start(bf16[32,1280]{1,0:T(8,128)(2,1)S(1)} %get-tuple-element.20), channel_id=1, source_target_pairs={{0,6},{1,7},{2,4},{3,5},{4,2},{5,3},{6,0},{7,1},{8,14},{9,15},{10,... | collective-permute-start | bytes 245768 | tf_op jit(solution)/shard_map/ppermute | solution.py:182
  23.9 1.2 %collective-permute-done.1.refs_1_ = bf16[32,1280]{1,0:T(8,128)(2,1)S(1)} collective-permute-done((bf16[32,1280]{1,0:T(8,128)(2,1)S(1)}, bf16[32,1280]{1,0:T(8,128)(2,1)S(1)}, u32[]{:S(2)}, u32[]{:S(2)}) %collective-permute-start.1) | collective-permute-done | bytes 81952 | tf_op jit(solution)/shard_map/ppermute | solution.py:182
  25.1 0.6 %collective-permute-done.2.refs_2_ = bf16[32,1280]{1,0:T(8,128)(2,1)S(1)} collective-permute-done((bf16[32,1280]{1,0:T(8,128)(2,1)S(1)}, bf16[32,1280]{1,0:T(8,128)(2,1)S(1)}, u32[]{:S(2)}, u32[]{:S(2)}) %collective-permute-start.2) | collective-permute-done | bytes 81952 | tf_op jit(solution)/shard_map/ppermute | solution.py:182
  25.7 2.4 %collective-permute-done.3.refs_3_ = bf16[32,1280]{1,0:T(8,128)(2,1)S(1)} collective-permute-done((bf16[32,1280]{1,0:T(8,128)(2,1)S(1)}, bf16[32,1280]{1,0:T(8,128)(2,1)S(1)}, u32[]{:S(2)}, u32[]{:S(2)}) %collective-permute-start.3) | collective-permute-done | bytes 81952 | tf_op jit(solution)/shard_map/ppermute | solution.py:182
  28.1 0.5 %collective-permute-start.4 = (bf16[32,1152]{1,0:T(8,128)(2,1)S(1)}, bf16[32,1152]{1,0:T(8,128)(2,1)S(1)}, u32[]{:S(2)}, u32[]{:S(2)}) collective-permute-start(bf16[32,1152]{1,0:T(8,128)(2,1)S(1)} %get-tuple-element.22), channel_id=1, source_target_pairs={{0,8},{1,9},{2,10},{3,11},{4,12},{5,13},{6,14},{7,15},{8,0},{9,1},... | collective-permute-start | bytes 221192 | tf_op jit(solution)/shard_map/ppermute | solution.py:182
  28.6 5.3 %collective-permute-done.4.got_ref = bf16[32,1152]{1,0:T(8,128)(2,1)S(1)} collective-permute-done((bf16[32,1152]{1,0:T(8,128)(2,1)S(1)}, bf16[32,1152]{1,0:T(8,128)(2,1)S(1)}, u32[]{:S(2)}, u32[]{:S(2)}) %collective-permute-start.4) | collective-permute-done | bytes 73760 | tf_op jit(solution)/shard_map/ppermute | solution.py:182
  33.9 0.0 collective-permute-done.5.swapped_ref
  33.9 0.0 copy-done.2
  33.9 0.0 copy-done.3
  34.0 0.6 %shard_map.96 = f32[32,128]{1,0:T(8,128)S(1)} custom-call(f32[32,1152]{1,0:T(8,128)S(1)} %get-tuple-element.21.mine_ref, bf16[32,1152]{1,0:T(8,128)(2,1)S(1)} %collective-permute-done.4.got_ref, bf16[8,64,1024]{2,1,0:T(8,128)(2,1)S(1)} %get-tuple-element.23.own_ref, bf16[8,64,1024]{2,1,0:T(8,128)(2,1)S(1)} %collective-permute-done.5.swapped_ref, ...), custom_call_target="tpu_custom_call" | custom-call | tf_op jit(solution)/shard_map/pallas_call | solution.py:24
  34.5 9.7 %all_to_all.11 = f32[32,1,128]{2,1,0:T(1,128)S(1)} all-to-all(f32[32,1,128]{2,1,0:T(1,128)S(1)} %bitcast.15), channel_id=1, replica_groups=mesh['section'=2,'dp'=16] {'section','dp'}, dimensions={0} | all-to-all | bytes 32768 | tf_op jit(solution)/shard_map/all_to_all | solution.py:19
  44.2 0.7 %shard_map.97 = f32[1,8,8]{2,1,0:T(8,128)} custom-call(f32[32,128]{1,0:T(8,128)S(1)} %bitcast.16, s32[1,4]{1,0:T(1,128)S(1)} %bitcast.18, f32[8,8]{1,0:T(8,128)S(1)} %copy-done.2), custom_call_target="tpu_custom_call" | custom-call | tf_op jit(solution)/shard_map/pallas_call | solution.py:24
  (3 shorter events, 0.1 us)
Async XLA Ops:
  0.0 16.5 %copy-start = (bf16[1,896,1024]{2,1,0:T(8,128)(2,1)S(1)}, bf16[1,896,1024]{2,1,0:T(8,128)(2,1)}, u32[]{:S(2)}) copy-start(bf16[1,896,1024]{2,1,0:T(8,128)(2,1)} %param.11) | copy-start | bytes 5505028
  0.0 17.0 %copy-start.1 = (bf16[1,256,1024]{2,1,0:T(8,128)(2,1)S(1)}, bf16[1,256,1024]{2,1,0:T(8,128)(2,1)}, u32[]{:S(2)}) copy-start(bf16[1,256,1024]{2,1,0:T(8,128)(2,1)} %param.12) | copy-start | bytes 1572868
  16.5 2.2 %copy-start.4 = (s32[4]{0:T(128)S(1)}, s32[4]{0:T(128)}, u32[]{:S(2)}) copy-start(s32[4]{0:T(128)} %param.15) | copy-start | bytes 52
  17.0 17.0 %copy-start.2 = (f32[8,8]{1,0:T(8,128)S(1)}, f32[8,8]{1,0:T(8,128)}, u32[]{:S(2)}) copy-start(f32[8,8]{1,0:T(8,128)} %prior_ref.1) | copy-start | bytes 772
  17.0 17.0 %copy-start.3 = (s32[4]{0:T(128)S(1)}, s32[4]{0:T(128)}, u32[]{:S(2)}) copy-start(s32[4]{0:T(128)} %param.16) | copy-start | bytes 52
  17.2 1.4 %collective-permute-start = (bf16[32,2048]{1,0:T(8,128)(2,1)S(1)}, bf16[32,2048]{1,0:T(8,128)(2,1)S(1)}, u32[]{:S(2)}, u32[]{:S(2)}) collective-permute-start(bf16[32,2048]{1,0:T(8,128)(2,1)S(1)} %get-tuple-element.16), channel_id=1, source_target_pairs={{0,1},{1,0},{2,3},{3,2},{4,5},{5,4},{6,7},{7,6},{8,9},{9,8},{10,11... | collective-permute-start | bytes 393224 | tf_op jit(solution)/shard_map/ppermute | solution.py:182
  20.2 13.7 %collective-permute-start.5 = (bf16[8,64,1024]{2,1,0:T(8,128)(2,1)S(1)}, bf16[8,64,1024]{2,1,0:T(8,128)(2,1)S(1)}, u32[]{:S(2)}, u32[]{:S(2)}) collective-permute-start(bf16[8,64,1024]{2,1,0:T(8,128)(2,1)S(1)} %get-tuple-element.23.own_ref), channel_id=1, source_target_pairs={{0,1},{1,0},{2,3},{3,2},{4,5},{5,4},{6,7},{7,6},{8,9},{9,8},{10,11... | collective-permute-start | bytes 3145736 | tf_op jit(solution)/shard_map/ppermute | solution.py:182
  20.4 4.7 %collective-permute-start.1 = (bf16[32,1280]{1,0:T(8,128)(2,1)S(1)}, bf16[32,1280]{1,0:T(8,128)(2,1)S(1)}, u32[]{:S(2)}, u32[]{:S(2)}) collective-permute-start(bf16[32,1280]{1,0:T(8,128)(2,1)S(1)} %get-tuple-element.18), channel_id=1, source_target_pairs={{0,2},{1,3},{2,0},{3,1},{4,6},{5,7},{6,4},{7,5},{8,10},{9,11},{10,... | collective-permute-start | bytes 245768 | tf_op jit(solution)/shard_map/ppermute | solution.py:182
  20.4 5.3 %collective-permute-start.2 = (bf16[32,1280]{1,0:T(8,128)(2,1)S(1)}, bf16[32,1280]{1,0:T(8,128)(2,1)S(1)}, u32[]{:S(2)}, u32[]{:S(2)}) collective-permute-start(bf16[32,1280]{1,0:T(8,128)(2,1)S(1)} %get-tuple-element.19), channel_id=1, source_target_pairs={{0,4},{1,5},{2,6},{3,7},{4,0},{5,1},{6,2},{7,3},{8,12},{9,13},{10,... | collective-permute-start | bytes 245768 | tf_op jit(solution)/shard_map/ppermute | solution.py:182
  21.1 7.0 %collective-permute-start.3 = (bf16[32,1280]{1,0:T(8,128)(2,1)S(1)}, bf16[32,1280]{1,0:T(8,128)(2,1)S(1)}, u32[]{:S(2)}, u32[]{:S(2)}) collective-permute-start(bf16[32,1280]{1,0:T(8,128)(2,1)S(1)} %get-tuple-element.20), channel_id=1, source_target_pairs={{0,6},{1,7},{2,4},{3,5},{4,2},{5,3},{6,0},{7,1},{8,14},{9,15},{10,... | collective-permute-start | bytes 245768 | tf_op jit(solution)/shard_map/ppermute | solution.py:182
  28.1 5.8 %collective-permute-start.4 = (bf16[32,1152]{1,0:T(8,128)(2,1)S(1)}, bf16[32,1152]{1,0:T(8,128)(2,1)S(1)}, u32[]{:S(2)}, u32[]{:S(2)}) collective-permute-start(bf16[32,1152]{1,0:T(8,128)(2,1)S(1)} %get-tuple-element.22), channel_id=1, source_target_pairs={{0,8},{1,9},{2,10},{3,11},{4,12},{5,13},{6,14},{7,15},{8,0},{9,1},... | collective-permute-start | bytes 221192 | tf_op jit(solution)/shard_map/ppermute | solution.py:182

commit v7 on v6

--- a/solution.py
+++ b/solution.py
@@ -139,7 +139,7 @@
         out_ref[at : at + 8] = line
 
 
-def table_kernel(per_section, queries, got_ref, rows_ref, prior_ref, out_ref):
+def table_kernel(per_section, queries, got_ref, rows_ref, prior_ref, out_hbm, table_ref, sem):
     sender = lax.broadcasted_iota(jnp.int32, got_ref.shape, 0) // per_section
     counted = sender <= lax.axis_index("section")
     depth = jnp.sum(jnp.where(counted, got_ref[...], 0.0), axis=0, keepdims=True)
@@ -150,7 +150,10 @@
         first = member * queries
         scores = jnp.broadcast_to(depth[:, first : first + queries], shape)
         table += jnp.where(rows_ref[:, member : member + 1] == own, scores, 0.0)
-    out_ref[0] = table
+    table_ref[0] = table
+    copy = pltpu.make_async_copy(table_ref, out_hbm, sem)
+    copy.start()
+    copy.wait()
 
 
 def packed_path(
@@ -254,13 +257,17 @@
         prior_table,
     )
     scores = exchange(spread.reshape(total, 1, LANES), ("section", "dp")).reshape(total, LANES)
-    return call(
+    return pl.pallas_call(
         functools.partial(table_kernel, n, query_proj.shape[1]),
-        jax.ShapeDtypeStruct((1,) + prior_table.shape, F32),
-        scores,
-        seq_rows,
-        prior_table,
-    )
+        out_shape=jax.ShapeDtypeStruct((1,) + prior_table.shape, F32),
+        in_specs=[VMEM] * 3,
+        out_specs=hbm,
+        scratch_shapes=[
+            pltpu.VMEM((1,) + prior_table.shape, F32),
+            pltpu.SemaphoreType.DMA,
+        ],
+        compiler_params=params,
+    )(scores, seq_rows, prior_table)
 
 
 def general_path(

time: 45.1 us -> 45.1 us (level)
    pallas_call x0 -> x1, Pallas kernels: none -> 0.74 us  [packed_path(): pl.pallas_call(functools.partial(table_kernel, n, query_proj.shape[1]), o...]
    pallas_call x5 -> x4, Pallas kernels: 1.58 us -> 0.85 us  [call(): pl.pallas_call(body, out_shape=out_shapes, in_specs=[VMEM] * len(operands...]
where the time goes in v7:
time: 45.1 us; the launch traced here: 44.9 us
  blocking collectives  25 us (55%)
  waiting for transfers between devices  10.8 us (24%)
  starting transfers between devices  4.3 us (10%)
  Pallas kernels  4.19 us (9%)
    all_to_all x2, blocking collectives, exchange(): return lax.all_to_all(pieces, axes, split_axis=0, concat_axis=0, tiled=True)  25 us
    ppermute x6, waiting for transfers between devices, swap(): return lax.ppermute(value, 'dp', [(i, i ^ bit) for i in range(n)])  10.8 us
    ppermute x6, starting transfers between devices, swap(): return lax.ppermute(value, 'dp', [(i, i ^ bit) for i in range(n)])  4.3 us
    pallas_call x1, Pallas kernels, packed_path(): prepare(lengths, *in_hbm(eigen_values[0], query_proj[0]), prepared)  1.52 us
    pallas_call x1, Pallas kernels, packed_path(): pl.pallas_call(pack_kernel, out_shape=jax.ShapeDtypeStruct((n, own_rows,...  1.08 us
  transfers between devices with their start and end apart: 6, of which 5 were waited for; matrix products, arithmetic and copies ran while one was open for 0% of the time, Pallas kernels for 0%

profile of v7, /device:TPU:0, one launch (start us, length us, event | category | flops | bytes accessed | tf_op | source)
XLA Modules:
  0.0 44.9 jit_solution(16499937392825534790)
XLA Ops:
  0.0 0.0 copy-start
  0.0 0.0 copy-start.1
  0.0 1.1 %shard_map.91 = bf16[16,4,1152]{2,1,0:T(4,128)(2,1)S(1)} custom-call(bf16[4,14336]{1,0:T(4,128)(2,1)} %bitcast.22, bf16[4,4096]{1,0:T(4,128)(2,1)} %bitcast.23), custom_call_target="tpu_custom_call" | custom-call | tf_op jit(solution)/shard_map/pallas_call | solution.py:187
  1.1 15.4 %all_to_all.10 = bf16[16,4,1152]{2,1,0:T(4,128)(2,1)S(1)} all-to-all(bf16[16,4,1152]{2,1,0:T(4,128)(2,1)S(1)} %shard_map.91), channel_id=1, replica_groups=mesh['section'=2,'dp'=16] {'dp'}, dimensions={0} | all-to-all | bytes 294912 | tf_op jit(solution)/shard_map/all_to_all | solution.py:19
  16.5 0.0 copy-done
  16.5 0.0 copy-start.4
  16.5 0.4 fusion.acts_ref
  17.0 0.0 copy-start.2
  17.0 0.0 copy-start.3
  17.0 0.0 copy-done.1
  17.0 0.2 shard_map.92
  17.2 0.1 collective-permute-start
  17.3 1.3 %collective-permute-done.refs_1_ = bf16[32,2048]{1,0:T(8,128)(2,1)S(1)} collective-permute-done((bf16[32,2048]{1,0:T(8,128)(2,1)S(1)}, bf16[32,2048]{1,0:T(8,128)(2,1)S(1)}, u32[]{:S(2)}, u32[]{:S(2)}) %collective-permute-start) | collective-permute-done | bytes 131104 | tf_op jit(solution)/shard_map/ppermute | solution.py:185
  18.7 0.0 copy-done.4
  18.7 1.5 %shard_map.95 = (bf16[8,64,1024]{2,1,0:T(8,128)(2,1)S(1)}, f32[32,128]{1,0:T(8,128)S(1)}) custom-call(s32[1,4]{1,0:T(1,128)S(1)} %bitcast.19, f32[64,1024]{1,0:T(8,128)} %bitcast.21, bf16[8,64,1024]{2,1,0:T(8,128)(2,1)} %bitcast.20, f32[32,1280]{1,0:T(8,128)S(1)} %get-tuple-element.17.refs_0_.after_ref), custom_call_target="tpu_custom_call" | custom-call | tf_op jit(solution)/shard_map/pallas_call | solution.py:245
  20.2 0.2 collective-permute-start.5
  20.4 0.0 collective-permute-start.1
  20.4 0.7 %collective-permute-start.2 = (bf16[32,1280]{1,0:T(8,128)(2,1)S(1)}, bf16[32,1280]{1,0:T(8,128)(2,1)S(1)}, u32[]{:S(2)}, u32[]{:S(2)}) collective-permute-start(bf16[32,1280]{1,0:T(8,128)(2,1)S(1)} %get-tuple-element.19), channel_id=1, source_target_pairs={{0,4},{1,5},{2,6},{3,7},{4,0},{5,1},{6,2},{7,3},{8,12},{9,13},{10,... | collective-permute-start | bytes 245768 | tf_op jit(solution)/shard_map/ppermute | solution.py:185
  21.1 2.8 %collective-permute-start.3 = (bf16[32,1280]{1,0:T(8,128)(2,1)S(1)}, bf16[32,1280]{1,0:T(8,128)(2,1)S(1)}, u32[]{:S(2)}, u32[]{:S(2)}) collective-permute-start(bf16[32,1280]{1,0:T(8,128)(2,1)S(1)} %get-tuple-element.20), channel_id=1, source_target_pairs={{0,6},{1,7},{2,4},{3,5},{4,2},{5,3},{6,0},{7,1},{8,14},{9,15},{10,... | collective-permute-start | bytes 245768 | tf_op jit(solution)/shard_map/ppermute | solution.py:185
  23.9 1.2 %collective-permute-done.1.refs_1_ = bf16[32,1280]{1,0:T(8,128)(2,1)S(1)} collective-permute-done((bf16[32,1280]{1,0:T(8,128)(2,1)S(1)}, bf16[32,1280]{1,0:T(8,128)(2,1)S(1)}, u32[]{:S(2)}, u32[]{:S(2)}) %collective-permute-start.1) | collective-permute-done | bytes 81952 | tf_op jit(solution)/shard_map/ppermute | solution.py:185
  25.1 0.6 %collective-permute-done.2.refs_2_ = bf16[32,1280]{1,0:T(8,128)(2,1)S(1)} collective-permute-done((bf16[32,1280]{1,0:T(8,128)(2,1)S(1)}, bf16[32,1280]{1,0:T(8,128)(2,1)S(1)}, u32[]{:S(2)}, u32[]{:S(2)}) %collective-permute-start.2) | collective-permute-done | bytes 81952 | tf_op jit(solution)/shard_map/ppermute | solution.py:185
  25.7 2.4 %collective-permute-done.3.refs_3_ = bf16[32,1280]{1,0:T(8,128)(2,1)S(1)} collective-permute-done((bf16[32,1280]{1,0:T(8,128)(2,1)S(1)}, bf16[32,1280]{1,0:T(8,128)(2,1)S(1)}, u32[]{:S(2)}, u32[]{:S(2)}) %collective-permute-start.3) | collective-permute-done | bytes 81952 | tf_op jit(solution)/shard_map/ppermute | solution.py:185
  28.1 0.5 %collective-permute-start.4 = (bf16[32,1152]{1,0:T(8,128)(2,1)S(1)}, bf16[32,1152]{1,0:T(8,128)(2,1)S(1)}, u32[]{:S(2)}, u32[]{:S(2)}) collective-permute-start(bf16[32,1152]{1,0:T(8,128)(2,1)S(1)} %get-tuple-element.22), channel_id=1, source_target_pairs={{0,8},{1,9},{2,10},{3,11},{4,12},{5,13},{6,14},{7,15},{8,0},{9,1},... | collective-permute-start | bytes 221192 | tf_op jit(solution)/shard_map/ppermute | solution.py:185
  28.6 5.3 %collective-permute-done.4.got_ref = bf16[32,1152]{1,0:T(8,128)(2,1)S(1)} collective-permute-done((bf16[32,1152]{1,0:T(8,128)(2,1)S(1)}, bf16[32,1152]{1,0:T(8,128)(2,1)S(1)}, u32[]{:S(2)}, u32[]{:S(2)}) %collective-permute-start.4) | collective-permute-done | bytes 73760 | tf_op jit(solution)/shard_map/ppermute | solution.py:185
  33.9 0.0 collective-permute-done.5.swapped_ref
  33.9 0.0 copy-done.2
  33.9 0.0 copy-done.3
  34.0 0.6 %shard_map.96 = f32[32,128]{1,0:T(8,128)S(1)} custom-call(f32[32,1152]{1,0:T(8,128)S(1)} %get-tuple-element.21.mine_ref, bf16[32,1152]{1,0:T(8,128)(2,1)S(1)} %collective-permute-done.4.got_ref, bf16[8,64,1024]{2,1,0:T(8,128)(2,1)S(1)} %get-tuple-element.23.own_ref, bf16[8,64,1024]{2,1,0:T(8,128)(2,1)S(1)} %collective-permute-done.5.swapped_ref, ...), custom_call_target="tpu_custom_call" | custom-call | tf_op jit(solution)/shard_map/pallas_call | solution.py:24
  34.5 9.7 %all_to_all.11 = f32[32,1,128]{2,1,0:T(1,128)S(1)} all-to-all(f32[32,1,128]{2,1,0:T(1,128)S(1)} %bitcast.15), channel_id=1, replica_groups=mesh['section'=2,'dp'=16] {'section','dp'}, dimensions={0} | all-to-all | bytes 32768 | tf_op jit(solution)/shard_map/all_to_all | solution.py:19
  44.2 0.7 %shard_map.97 = f32[1,8,8]{2,1,0:T(8,128)} custom-call(f32[32,128]{1,0:T(8,128)S(1)} %bitcast.16, s32[1,4]{1,0:T(1,128)S(1)} %bitcast.18, f32[8,8]{1,0:T(8,128)S(1)} %copy-done.2), custom_call_target="tpu_custom_call" | custom-call | tf_op jit(solution)/shard_map/pallas_call | solution.py:260
  (3 shorter events, 0.1 us)
Async XLA Ops:
  0.0 16.5 %copy-start = (bf16[1,896,1024]{2,1,0:T(8,128)(2,1)S(1)}, bf16[1,896,1024]{2,1,0:T(8,128)(2,1)}, u32[]{:S(2)}) copy-start(bf16[1,896,1024]{2,1,0:T(8,128)(2,1)} %param.11) | copy-start | bytes 5505028
  0.0 17.0 %copy-start.1 = (bf16[1,256,1024]{2,1,0:T(8,128)(2,1)S(1)}, bf16[1,256,1024]{2,1,0:T(8,128)(2,1)}, u32[]{:S(2)}) copy-start(bf16[1,256,1024]{2,1,0:T(8,128)(2,1)} %param.12) | copy-start | bytes 1572868
  16.5 2.2 %copy-start.4 = (s32[4]{0:T(128)S(1)}, s32[4]{0:T(128)}, u32[]{:S(2)}) copy-start(s32[4]{0:T(128)} %param.15) | copy-start | bytes 52
  17.0 17.0 %copy-start.2 = (f32[8,8]{1,0:T(8,128)S(1)}, f32[8,8]{1,0:T(8,128)}, u32[]{:S(2)}) copy-start(f32[8,8]{1,0:T(8,128)} %prior_ref.1) | copy-start | bytes 772
  17.0 17.0 %copy-start.3 = (s32[4]{0:T(128)S(1)}, s32[4]{0:T(128)}, u32[]{:S(2)}) copy-start(s32[4]{0:T(128)} %param.16) | copy-start | bytes 52
  17.2 1.4 %collective-permute-start = (bf16[32,2048]{1,0:T(8,128)(2,1)S(1)}, bf16[32,2048]{1,0:T(8,128)(2,1)S(1)}, u32[]{:S(2)}, u32[]{:S(2)}) collective-permute-start(bf16[32,2048]{1,0:T(8,128)(2,1)S(1)} %get-tuple-element.16), channel_id=1, source_target_pairs={{0,1},{1,0},{2,3},{3,2},{4,5},{5,4},{6,7},{7,6},{8,9},{9,8},{10,11... | collective-permute-start | bytes 393224 | tf_op jit(solution)/shard_map/ppermute | solution.py:185
  20.2 13.7 %collective-permute-start.5 = (bf16[8,64,1024]{2,1,0:T(8,128)(2,1)S(1)}, bf16[8,64,1024]{2,1,0:T(8,128)(2,1)S(1)}, u32[]{:S(2)}, u32[]{:S(2)}) collective-permute-start(bf16[8,64,1024]{2,1,0:T(8,128)(2,1)S(1)} %get-tuple-element.23.own_ref), channel_id=1, source_target_pairs={{0,1},{1,0},{2,3},{3,2},{4,5},{5,4},{6,7},{7,6},{8,9},{9,8},{10,11... | collective-permute-start | bytes 3145736 | tf_op jit(solution)/shard_map/ppermute | solution.py:185
  20.4 4.7 %collective-permute-start.1 = (bf16[32,1280]{1,0:T(8,128)(2,1)S(1)}, bf16[32,1280]{1,0:T(8,128)(2,1)S(1)}, u32[]{:S(2)}, u32[]{:S(2)}) collective-permute-start(bf16[32,1280]{1,0:T(8,128)(2,1)S(1)} %get-tuple-element.18), channel_id=1, source_target_pairs={{0,2},{1,3},{2,0},{3,1},{4,6},{5,7},{6,4},{7,5},{8,10},{9,11},{10,... | collective-permute-start | bytes 245768 | tf_op jit(solution)/shard_map/ppermute | solution.py:185
  20.4 5.3 %collective-permute-start.2 = (bf16[32,1280]{1,0:T(8,128)(2,1)S(1)}, bf16[32,1280]{1,0:T(8,128)(2,1)S(1)}, u32[]{:S(2)}, u32[]{:S(2)}) collective-permute-start(bf16[32,1280]{1,0:T(8,128)(2,1)S(1)} %get-tuple-element.19), channel_id=1, source_target_pairs={{0,4},{1,5},{2,6},{3,7},{4,0},{5,1},{6,2},{7,3},{8,12},{9,13},{10,... | collective-permute-start | bytes 245768 | tf_op jit(solution)/shard_map/ppermute | solution.py:185
  21.1 7.0 %collective-permute-start.3 = (bf16[32,1280]{1,0:T(8,128)(2,1)S(1)}, bf16[32,1280]{1,0:T(8,128)(2,1)S(1)}, u32[]{:S(2)}, u32[]{:S(2)}) collective-permute-start(bf16[32,1280]{1,0:T(8,128)(2,1)S(1)} %get-tuple-element.20), channel_id=1, source_target_pairs={{0,6},{1,7},{2,4},{3,5},{4,2},{5,3},{6,0},{7,1},{8,14},{9,15},{10,... | collective-permute-start | bytes 245768 | tf_op jit(solution)/shard_map/ppermute | solution.py:185
  28.1 5.8 %collective-permute-start.4 = (bf16[32,1152]{1,0:T(8,128)(2,1)S(1)}, bf16[32,1152]{1,0:T(8,128)(2,1)S(1)}, u32[]{:S(2)}, u32[]{:S(2)}) collective-permute-start(bf16[32,1152]{1,0:T(8,128)(2,1)S(1)} %get-tuple-element.22), channel_id=1, source_target_pairs={{0,8},{1,9},{2,10},{3,11},{4,12},{5,13},{6,14},{7,15},{8,0},{9,1},... | collective-permute-start | bytes 221192 | tf_op jit(solution)/shard_map/ppermute | solution.py:185
